TPU v7x, 256 devices: a whole 4x4x8 slice. The times are simulated.
256 devices in a mesh: grid: 8 (over z), orb: 16 (over y, x_hi, core), pts: 2 (over x_lo).
Axes of the slice: x: 4 (x_hi: 2, x_lo: 2; x = x_hi * 2 + x_lo), y: 4, z: 8, core: 2. Of those that a mesh axis runs over, the one named last changes fastest.
Arguments:
- orbitals: bfloat16 [2048, 2048], P('grid', 'orb'), may hold values from -6 to 6
- points: int32 [8192], replicated, may hold values from 0 to 2047
- fitting: bfloat16 [2048, 8192], P('grid', ('orb', 'pts')), may hold values from -0.0625 to 0.0625
- screened: bfloat16 [8192, 8192], P(('orb', 'pts'), 'grid'), may hold values from -0.0014648438 to 0.0014648438
Outputs:
- exchange_orbitals: float32 [2048, 2048], P(('orb', 'pts'), 'grid')
- exchange_matrix: float32 [2048, 2048], P(('orb', 'pts'), 'grid')
Inputs may be any that keep to these rules, and one draw needn't show every extreme that they name: Grid rows of the window; two points may name the same row.
All inputs are finite; a program needn't handle non-finite values.
Results may differ from a plain program's by a relative error of at most 0.005.
Values may be sent and summed in bfloat16 or wider, within the bound.
No kernel may reach another device: no remote copies, remote signals or barrier semaphores. Data moves between devices by JAX's collectives and lax.ppermute only.
A program may use at most 128 MiB of HBM per device.

v0:
```python
import math

import jax
import jax.numpy as jnp
from jax import lax
from jax.experimental import pallas as pl
from jax.experimental.pallas import tpu as pltpu
from jax.sharding import Mesh, PartitionSpec as P


BF = jnp.bfloat16
F32 = jnp.float32
ORB = ("y", "xh", "core")
PLANE = ("y", "xh", "core", "pts")
CHIPS = ("y", "xh", "pts")
X = ("xh", "pts")


def sent_to_all(x, axis):
    copies = jnp.broadcast_to(x, (lax.axis_size(axis), *x.shape))
    return lax.all_to_all(copies, axis, split_axis=0, concat_axis=0, tiled=True)


def from_next(x, step):
    n = lax.axis_size("y")
    return lax.ppermute(x, "y", [(i, (i - step) % n) for i in range(n)])


def with_twin(x):
    return lax.ppermute(x, X, [(0, 1), (1, 0), (2, 3), (3, 2)])


def with_mirror(x):
    return lax.ppermute(x, X, [(0, 3), (3, 0), (1, 2), (2, 1)])


def with_far(x):
    return lax.ppermute(x, X, [(0, 2), (2, 0), (1, 3), (3, 1)])


def along_y(first, second):
    after, before = from_next(first, 1), from_next(first, -1)
    after2, before2 = from_next(second, 1), from_next(second, -1)
    far, far2 = from_next(after, 1), from_next(before2, -1)
    return (first, after, far, before), (second, after2, far2, before2)


def along_x(first, second):
    twin, mirror = with_twin(first), with_mirror(first)
    twin2, mirror2 = with_twin(second), with_mirror(second)
    far, far2 = with_twin(mirror), with_mirror(twin2)
    return (first, twin, mirror, far), (second, twin2, mirror2, far2)


def other_core(x):
    return lax.ppermute(x, "core", [(0, 1), (1, 0)])


def pick_kernel(choose_ref, *refs):
    pieces, outs = refs[:-4], refs[-4:]
    own_ref, other_ref, picked_ref, columns_ref = outs
    step = pl.program_id(0)
    rows = own_ref.shape[0]
    height, width = pieces[0].shape[1:]
    alpha, beta = pieces[:8], pieces[8:]

    @pl.when(step == 0)
    def _():
        own_ref[...] = jnp.zeros_like(own_ref)
        other_ref[...] = jnp.zeros_like(other_ref)

    for at in range(4):

        @pl.when(step == at)
        def _():
            for col, roles in enumerate(((0, 1), (3, 2))):
                for k, role in enumerate(roles):
                    for part, piece in enumerate(
                        (alpha[role + 4 * (at // 2)][at % 2], beta[at + 4 * (role // 2)][role % 2])
                    ):
                        top = (2 * k + part) * height
                        columns_ref[0, top : top + height, col * width : (col + 1) * width] = piece

    picked = jnp.dot(choose_ref[...], columns_ref[0], preferred_element_type=F32).astype(BF)
    picked_ref[...] = picked[2 * rows :]
    for k, out in enumerate((own_ref, other_ref)):
        out[...] += lax.dot_general(
            picked[k * rows : (k + 1) * rows],
            picked[2 * rows :],
            (((1,), (1,)), ((), ())),
            preferred_element_type=F32,
        )


def pick(choose, pieces, rows):
    _, height, width = pieces[0].shape
    total, nrows = choose.shape
    rest = total - 2 * rows
    whole = lambda i: (0, 0)
    return pl.pallas_call(
        pick_kernel,
        grid=(4,),
        in_specs=[pl.BlockSpec((total, nrows), whole)]
        + [pl.BlockSpec((2, height, width), lambda i: (0, 0, 0))] * len(pieces),
        out_specs=[
            pl.BlockSpec((rows, rest), whole),
            pl.BlockSpec((rows, rest), whole),
            pl.BlockSpec((rest, 2 * width), lambda i: (0, i)),
            pl.BlockSpec((1, nrows, 2 * width), lambda i: (i, 0, 0)),
        ],
        out_shape=[
            jax.ShapeDtypeStruct((rows, rest), F32),
            jax.ShapeDtypeStruct((rows, rest), F32),
            jax.ShapeDtypeStruct((rest, 8 * width), BF),
            jax.ShapeDtypeStruct((4, nrows, 2 * width), BF),
        ],
        compiler_params=pltpu.CompilerParams(dimension_semantics=("arbitrary",), vmem_limit_bytes=30 << 20),
        cost_estimate=pl.CostEstimate(
            flops=16 * width * (total * nrows + 2 * rows * rest),
            bytes_accessed=16 * nrows * width,
            transcendentals=0,
        ),
        name="pick",
    )(choose, *pieces)


def body(orbitals, points, fitting, screened):
    n_grid = lax.axis_size("grid")
    n_plane = lax.axis_size(PLANE)
    grid_index = lax.axis_index("grid")
    plane_index = lax.axis_index(PLANE)
    y, xh, core, pts = (lax.axis_index(a) for a in PLANE)
    rows_dev, width = orbitals.shape
    nrows = rows_dev * n_grid
    nfull = width * lax.axis_size(ORB)
    npoints = points.shape[0]
    row_block = npoints // n_plane
    column_block = npoints // n_grid
    share = nfull // (n_plane * n_grid)
    part = rows_dev // 2
    quarter = nrows // 4

    own_rows = lax.dynamic_slice_in_dim(orbitals, pts * part, part, 0)
    held = sent_to_all(own_rows, "grid").reshape(2, quarter, width)
    alpha, beta = held[0], held[1]
    alphas = [alpha, from_next(alpha, 1), from_next(alpha, 2), from_next(alpha, -1)]
    betas = [beta, with_twin(beta), with_mirror(beta), with_far(beta)]
    a_first, a_second = jnp.stack(alphas[:2]), jnp.stack(alphas[2:])
    b_first, b_second = jnp.stack(betas[:2]), jnp.stack(betas[2:])
    pieces = [x for part in along_x(a_first, a_second) + along_y(b_first, b_second) for x in part]

    fit_own = sent_to_all(fitting, "grid").reshape(nrows, row_block)
    fit_other = other_core(fit_own)

    near = lax.broadcasted_iota(jnp.int32, (nrows,), 0)
    half_of = lax.rem(near // (nrows // 2) + pts, 2)
    within = lax.rem(near, nrows // 2)
    ids = (within // part) * rows_dev + half_of * part + lax.rem(within, part)
    mine = lax.dynamic_slice_in_dim(points, plane_index * row_block, row_block, 0)
    theirs_index = plane_index + (1 - 2 * core) * lax.axis_size("pts")
    theirs = lax.dynamic_slice_in_dim(points, theirs_index * row_block, row_block, 0)
    block = lax.dynamic_slice_in_dim(points, grid_index * column_block, column_block, 0)
    wanted = jnp.concatenate([mine, theirs, block])
    choose = (wanted[:, None] == ids[None]).astype(BF)
    density, density_other, picked, columns = pick(choose, pieces, row_block)

    density = density + other_core(density_other)
    masked = (density * screened.astype(F32)).astype(BF)
    masked, fit_own = lax.optimization_barrier((masked, fit_own))
    masked_other = other_core(masked)

    def applied_by(masked):
        partial = lax.dot_general(
            picked, masked, (((0,), (1,)), ((), ())), preferred_element_type=F32
        ).astype(BF)
        partial = partial.reshape(-1, n_grid, share, row_block)
        return partial.transpose(1, 0, 2, 3)

    partial = jnp.stack([applied_by(masked), applied_by(masked_other)], axis=1)
    parts = lax.all_to_all(partial, "grid", 0, 0, tiled=True)
    applied = jnp.sum(parts.astype(F32), axis=0).astype(BF)
    applied = applied.reshape(2, 4, 2, 2 * share, row_block)
    applied = jnp.where(xh == 0, applied, applied[:, :, ::-1])
    applied = lax.dynamic_slice_in_dim(
        jnp.concatenate([applied, applied], axis=1), lax.rem(4 - y, 4), 4, 1
    ).reshape(2, -1, row_block)
    terms = sum(
        lax.dot_general(a, f, (((1,), (1,)), ((), ())), preferred_element_type=F32)
        for a, f in ((applied[0], fit_own), (applied[1], fit_other))
    ).astype(BF)
    parts = lax.all_to_all(terms.reshape(-1, share, nrows), CHIPS, 0, 0, tiled=True)
    exchange = -jnp.sum(parts.astype(F32), axis=0)
    exchange = jnp.stack([exchange, other_core(exchange)])
    exchange = jnp.where(core == 0, exchange, exchange[::-1])

    halves = exchange.astype(BF).reshape(2 * share, n_grid, 2, part)
    halves = jnp.where(pts == 0, halves, halves[:, :, ::-1])
    halves = halves.transpose(0, 2, 1, 3).reshape(2 * share, nrows)
    matrix = lax.dot_general(
        halves, columns, (((1,), (1,)), ((), ())), preferred_element_type=F32
    ) / math.sqrt(nrows)
    matrix = matrix.transpose(1, 0, 2).reshape(4, 2 * share, 2, width).transpose(0, 2, 1, 3)
    matrix = jnp.where(xh == 0, matrix, matrix[:, ::-1])
    matrix = lax.dynamic_slice_in_dim(
        jnp.concatenate([matrix, matrix]), lax.rem(4 - y, 4), 4, 0
    ).reshape(n_grid, 2, share, width)
    mine = exchange.reshape(2, share, n_grid, 2, width)
    mine = lax.dynamic_index_in_dim(mine, core, 3, keepdims=False).transpose(2, 0, 1, 3)
    both = jnp.stack([mine, matrix], axis=2).reshape(2 * n_grid, 2, share, width)
    both = lax.all_to_all(both, ("grid", "core"), 0, 0, tiled=True)
    both = both.reshape(n_grid, 2, 2, share, width).transpose(2, 0, 3, 1, 4)
    both = both.reshape(2, n_grid * share, 2 * width)
    return both[0], both[1]


def solution(mesh):
    n_grid, n_orb, n_pts = (mesh.shape[a] for a in ("grid", "orb", "pts"))
    fine = Mesh(
        mesh.devices.reshape(n_grid, n_orb // 4, 2, 2, n_pts),
        ("grid", "y", "xh", "core", "pts"),
    )
    in_specs = (P("grid", ORB), P(), P("grid", PLANE), P(PLANE, "grid"))
    out_specs = (P(PLANE, "grid"), P(PLANE, "grid"))
    return jax.shard_map(body, mesh=fine, in_specs=in_specs, out_specs=out_specs, check_vma=False)
```

profile of v0, /device:TPU:1, one launch (start us, length us, event | category | flops | bytes accessed | tf_op | source)
XLA Modules:
  0.0 163.7 jit_solution(10602596947310859711)
XLA Ops:
  0.6 0.0 copy-start
  0.6 0.8 copy-done
  1.5 19.3 %all_to_all.25 = bf16[8,128,128]{2,1,0:T(8,128)(2,1)S(1)} all-to-all(bf16[8,128,128]{2,1,0:T(8,128)(2,1)S(1)} %broadcast_in_dim.8), channel_id=1, replica_groups=mesh['grid'=8,'y'=4,'xh'=2,'core'=2,'pts'=2] {'grid'}, dimensions={0} | all-to-all | bytes 524288 | tf_op jit(solution)/shard_map/all_to_all | solution.py:21
  20.8 2.6 %collective-permute-start.13 = (bf16[512,128]{1,0:T(8,128)(2,1)S(1)}, bf16[512,128]{1,0:T(8,128)(2,1)S(1)}, u32[]{:S(2)}, u32[]{:S(2)}) collective-permute-start(bf16[512,128]{1,0:T(8,128)(2,1)S(1)} %bitcast.68), channel_id=1, source_target_pairs={{0,5},{5,0},{1,4},{4,1},{2,7},{7,2},{3,6},{6,3},{8,13},{13,8},{9,1... | collective-permute-start | bytes 393224 | tf_op jit(solution)/shard_map/ppermute | solution.py:34
  23.4 0.5 collective-permute-start.14
  23.9 2.9 %collective-permute-start.4 = (bf16[512,128]{1,0:T(8,128)(2,1)S(1)}, bf16[512,128]{1,0:T(8,128)(2,1)S(1)}, u32[]{:S(2)}, u32[]{:S(2)}) collective-permute-start(bf16[512,128]{1,0:T(8,128)(2,1)S(1)} %bitcast.72), channel_id=1, source_target_pairs={{0,16},{8,24},{16,0},{24,8},{1,17},{9,25},{17,1},{25,9},{2,18},{10... | collective-permute-start | bytes 393224 | tf_op jit(solution)/shard_map/ppermute | solution.py:26
  26.8 0.4 collective-permute-start.5
  27.2 2.3 %collective-permute-start = (bf16[512,128]{1,0:T(8,128)(2,1)S(1)}, bf16[512,128]{1,0:T(8,128)(2,1)S(1)}, u32[]{:S(2)}, u32[]{:S(2)}) collective-permute-start(bf16[512,128]{1,0:T(8,128)(2,1)S(1)} %bitcast.74), channel_id=1, source_target_pairs={{0,24},{8,0},{16,8},{24,16},{1,25},{9,1},{17,9},{25,17},{2,26},{10... | collective-permute-start | bytes 393224 | tf_op jit(solution)/shard_map/ppermute | solution.py:26
  29.5 0.0 collective-permute-done.13
  29.5 0.0 collective-permute-done.14
  29.6 0.7 collective-permute-start.16
  30.2 3.0 %collective-permute-done.5 = bf16[512,128]{1,0:T(8,128)(2,1)S(1)} collective-permute-done((bf16[512,128]{1,0:T(8,128)(2,1)S(1)}, bf16[512,128]{1,0:T(8,128)(2,1)S(1)}, u32[]{:S(2)}, u32[]{:S(2)}) %collective-permute-start.5) | collective-permute-done | bytes 131104 | tf_op jit(solution)/shard_map/ppermute | solution.py:26
  33.3 0.3 collective-permute-start.6
  33.6 1.2 collective-permute-start.9
  34.9 2.1 %broadcast_in_dim.9 = bf16[8,256,256]{2,1,0:T(8,128)(2,1)} broadcast(bf16[256,256]{1,0:T(8,128)(2,1)} %param.6), dimensions={1,2} | broadcast | bytes 1179648 | tf_op jit(solution)/shard_map/broadcast_in_dim | solution.py:20
  36.9 4.2 %all-to-all-start.1 = ((bf16[8,256,256]{2,1,0:T(8,128)(2,1)}), bf16[8,256,256]{2,1,0:T(8,128)(2,1)}, u32[]{:S(2)}, u32[]{:S(2)}) async-start(bf16[8,256,256]{2,1,0:T(8,128)(2,1)} %broadcast_in_dim.9), calls=%async_computation.1 | async-start | bytes 2097152 | tf_op jit(solution)/shard_map/all_to_all | solution.py:21
  41.2 0.1 collective-permute-start.15
  41.3 1.9 %collective-permute-start.7 = (bf16[2,512,128]{2,1,0:T(8,128)(2,1)S(1)}, bf16[2,512,128]{2,1,0:T(8,128)(2,1)S(1)}, u32[]{:S(2)}, u32[]{:S(2)}) collective-permute-start(bf16[2,512,128]{2,1,0:T(8,128)(2,1)S(1)} %pad_maximum_fusion.2.refs_4_), channel_id=1, source_target_pairs={{0,5},{5,0},{1,4},{4,1},{2,7},{7,2},{3,6},{6,3},{8,13},{13,8},{9,1... | collective-permute-start | bytes 786440 | tf_op jit(solution)/shard_map/ppermute | solution.py:34
  43.2 0.9 collective-permute-start.2
  44.2 0.1 collective-permute-start.1
  44.3 0.1 collective-permute-start.10
  44.4 0.8 fusion.21
  45.3 0.7 dynamic_slice.24
  46.0 0.5 collective-permute-done.15.refs_13_
  46.5 1.0 collective-permute-start.12
  47.5 0.3 collective-permute-done.7.refs_6_
  47.8 1.4 collective-permute-start.17
  49.2 1.5 collective-permute-done.10.refs_9_
  50.6 1.8 %collective-permute-start.8 = (bf16[2,512,128]{2,1,0:T(8,128)(2,1)S(1)}, bf16[2,512,128]{2,1,0:T(8,128)(2,1)S(1)}, u32[]{:S(2)}, u32[]{:S(2)}) collective-permute-start(bf16[2,512,128]{2,1,0:T(8,128)(2,1)S(1)} %collective-permute-done.6.refs_5_), channel_id=1, source_target_pairs={{0,5},{5,0},{1,4},{4,1},{2,7},{7,2},{3,6},{6,3},{8,13},{13,8},{9,1... | collective-permute-start | bytes 786440 | tf_op jit(solution)/shard_map/ppermute | solution.py:34
  52.5 1.4 collective-permute-start.11
  53.8 1.3 collective-permute-start.3
  55.2 1.1 compare_convert_fusion.choose_ref
  56.2 0.0 copy-start.4
  56.3 3.2 %collective-permute-done.8.refs_7_ = bf16[2,512,128]{2,1,0:T(8,128)(2,1)S(1)} collective-permute-done((bf16[2,512,128]{2,1,0:T(8,128)(2,1)S(1)}, bf16[2,512,128]{2,1,0:T(8,128)(2,1)S(1)}, u32[]{:S(2)}, u32[]{:S(2)}) %collective-permute-start.8) | collective-permute-done | bytes 262176 | tf_op jit(solution)/shard_map/ppermute | solution.py:34
  59.4 0.0 collective-permute-done.3.refs_3_
  59.5 11.5 %pick.1 = (f32[256,1024]{1,0:T(8,128)S(1)}, f32[256,1024]{1,0:T(8,128)S(1)}, bf16[1024,1024]{1,0:T(8,128)(2,1)S(1)}, bf16[4,2048,256]{2,1,0:T(8,128)(2,1)S(1)}) custom-call(bf16[1536,2048]{1,0:T(8,128)(2,1)S(1)} %compare_convert_fusion.choose_ref, bf16[2,512,128]{2,1,0:T(8,128)(2,1)S(1)} %pad_maximum_fusion.1.refs_0_, ...), custom_call_target="tpu_custom_call" | custom-call | flops 7516192768 | bytes 4194304 | tf_op jit(solution)/shard_map/pick/pallas_call | solution.py:100
  71.0 1.9 %copy-done.1 = bf16[4,2048,256]{2,1,0:T(8,128)(2,1)} copy-done((bf16[4,2048,256]{2,1,0:T(8,128)(2,1)}, bf16[4,2048,256]{2,1,0:T(8,128)(2,1)S(1)}, u32[]{:S(2)}) %copy-start.1) | copy-done | bytes 4194328
  72.9 1.4 copy-done.2
  74.3 9.2 %collective-permute-start.18 = (f32[256,1024]{1,0:T(8,128)S(1)}, f32[256,1024]{1,0:T(8,128)S(1)}, u32[]{:S(2)}, u32[]{:S(2)}) collective-permute-start(f32[256,1024]{1,0:T(8,128)S(1)} %get-tuple-element.10), channel_id=1, source_target_pairs={{0,2},{2,0},{1,3},{3,1},{4,6},{6,4},{5,7},{7,5},{8,10},{10,8},{9,1... | collective-permute-start | bytes 3145736 | tf_op jit(solution)/shard_map/ppermute | solution.py:56
  83.5 2.3 %collective-permute-done.18 = f32[256,1024]{1,0:T(8,128)S(1)} collective-permute-done((f32[256,1024]{1,0:T(8,128)S(1)}, f32[256,1024]{1,0:T(8,128)S(1)}, u32[]{:S(2)}, u32[]{:S(2)}) %collective-permute-start.18) | collective-permute-done | bytes 1048608 | tf_op jit(solution)/shard_map/ppermute | solution.py:56
  85.8 0.3 multiply_convert_fusion
  86.1 0.5 collective-permute-start.19
  86.6 2.3 %convolution_convert_fusion.1 = bf16[1024,256]{1,0:T(8,128)(2,1)S(1)} fusion(bf16[1024,1024]{1,0:T(8,128)(2,1)} %copy-done.2, bf16[256,1024]{1,0:T(8,128)(2,1)S(1)} %multiply_convert_fusion), kind=kOutput, calls=%fused_computation.5 | convolution fusion | flops 537133056 | bytes 3145728 | tf_op jit(solution)/shard_map/dot_general | solution.py:173
  88.9 0.8 convolution_convert_fusion
  89.7 0.1 copy_bitcast_fusion
  89.8 1.1 pad_maximum_fusion
  90.9 6.9 %all-to-all-start.2 = ((bf16[8,2,16,8,256]{4,3,2,1,0:T(8,128)(2,1)}), bf16[8,2,16,8,256]{4,3,2,1,0:T(8,128)(2,1)S(1)}, u32[]{:S(2)}, u32[]{:S(2)}) async-start(bf16[8,2,16,8,256]{4,3,2,1,0:T(8,128)(2,1)} %pad_maximum_fusion), calls=%async_computation.2 | async-start | bytes 2097152 | tf_op jit(solution)/shard_map/all_to_all | solution.py:180
  97.8 0.5 collective-permute-start.20
  98.3 28.7 %all-to-all-done.2 = bf16[8,2,16,8,256]{4,3,2,1,0:T(8,128)(2,1)S(1)} async-done(((bf16[8,2,16,8,256]{4,3,2,1,0:T(8,128)(2,1)}), bf16[8,2,16,8,256]{4,3,2,1,0:T(8,128)(2,1)S(1)}, u32[]{:S(2)}, u32[]{:S(2)}) %all-to-all-start.2) | async-done | bytes 1048608 | tf_op jit(solution)/shard_map/all_to_all | solution.py:180
  127.1 0.1 reduce_sum.21
  127.3 0.1 fusion.3
  127.3 1.7 %fusion.22 = f32[128,2048]{1,0:T(8,128)S(1)} fusion(bf16[128,256]{1,0:T(8,128)(2,1)S(1)} %bitcast.76, bf16[2048,256]{1,0:T(8,128)(2,1)} %bitcast.10), kind=kOutput, calls=%fused_computation.64 | convolution fusion | flops 134217728 | bytes 2162688 | tf_op jit(solution)/shard_map/dot_general | solution.py:188
  129.1 0.5 fusion.1
  129.5 14.9 %all_to_all.26 = bf16[16,8,2048]{2,1,0:T(8,128)(2,1)S(1)} all-to-all(bf16[16,8,2048]{2,1,0:T(8,128)(2,1)S(1)} %fusion.1), channel_id=1, replica_groups=mesh['grid'=8,'y'=4,'xh'=2,'core'=2,'pts'=2] {'y','xh','pts'}, dimensions={0} | all-to-all | bytes 1048576 | tf_op jit(solution)/shard_map/all_to_all | solution.py:191
  144.4 0.1 convert_reduce_fusion
  144.5 2.0 %collective-permute-start.21 = (f32[8,2048]{1,0:T(8,128)S(1)}, f32[8,2048]{1,0:T(8,128)S(1)}, u32[]{:S(2)}, u32[]{:S(2)}) collective-permute-start(f32[8,2048]{1,0:T(8,128)S(1)} %get-tuple-element.23), channel_id=1, source_target_pairs={{0,2},{2,0},{1,3},{3,1},{4,6},{6,4},{5,7},{7,5},{8,10},{10,8},{9,1... | collective-permute-start | bytes 196616 | tf_op jit(solution)/shard_map/ppermute | solution.py:56
  146.5 0.9 collective-permute-done.21
  147.5 0.3 rev.14
  147.8 0.1 fusion.4
  147.9 2.8 %fusion.2 = f32[4,2,2,8,128]{4,3,2,1,0:T(8,128)S(1)} fusion(bf16[16,2048,1]{1,0,2:T(8,128)(2,1)S(1)} %reshape.112, bf16[4,2048,256]{2,1,0:T(8,128)(2,1)} %copy-done.1), kind=kOutput, calls=%fused_computation.7 | convolution fusion | flops 67125248 | bytes 4325376 | tf_op jit(solution)/shard_map/dot_general | solution.py:199
  150.8 0.1 reshape.107
  150.9 0.1 constant_dynamic-slice_fusion
  151.1 11.9 %all_to_all.27 = f32[16,2,8,128]{3,2,1,0:T(8,128)S(1)} all-to-all(f32[16,2,8,128]{3,2,1,0:T(8,128)S(1)} %copy.17), channel_id=1, replica_groups=mesh['grid'=8,'y'=4,'xh'=2,'core'=2,'pts'=2] {'grid','core'}, dimensions={0} | all-to-all | bytes 262144 | tf_op jit(solution)/shard_map/all_to_all | solution.py:210
  163.0 0.7 slice_bitcast_fusion
  (41 shorter events, 0.5 us)
Async XLA Ops:
  0.6 0.8 copy-start
  20.8 8.7 %collective-permute-start.13 = (bf16[512,128]{1,0:T(8,128)(2,1)S(1)}, bf16[512,128]{1,0:T(8,128)(2,1)S(1)}, u32[]{:S(2)}, u32[]{:S(2)}) collective-permute-start(bf16[512,128]{1,0:T(8,128)(2,1)S(1)} %bitcast.68), channel_id=1, source_target_pairs={{0,5},{5,0},{1,4},{4,1},{2,7},{7,2},{3,6},{6,3},{8,13},{13,8},{9,1... | collective-permute-start | bytes 393224 | tf_op jit(solution)/shard_map/ppermute | solution.py:34
  23.4 6.1 %collective-permute-start.14 = (bf16[512,128]{1,0:T(8,128)(2,1)S(1)}, bf16[512,128]{1,0:T(8,128)(2,1)S(1)}, u32[]{:S(2)}, u32[]{:S(2)}) collective-permute-start(bf16[512,128]{1,0:T(8,128)(2,1)S(1)} %bitcast.69), channel_id=1, source_target_pairs={{0,4},{4,0},{1,5},{5,1},{2,6},{6,2},{3,7},{7,3},{8,12},{12,8},{9,1... | collective-permute-start | bytes 393224 | tf_op jit(solution)/shard_map/ppermute | solution.py:38
  23.9 6.3 %collective-permute-start.4 = (bf16[512,128]{1,0:T(8,128)(2,1)S(1)}, bf16[512,128]{1,0:T(8,128)(2,1)S(1)}, u32[]{:S(2)}, u32[]{:S(2)}) collective-permute-start(bf16[512,128]{1,0:T(8,128)(2,1)S(1)} %bitcast.72), channel_id=1, source_target_pairs={{0,16},{8,24},{16,0},{24,8},{1,17},{9,25},{17,1},{25,9},{2,18},{10... | collective-permute-start | bytes 393224 | tf_op jit(solution)/shard_map/ppermute | solution.py:26
  26.8 6.4 %collective-permute-start.5 = (bf16[512,128]{1,0:T(8,128)(2,1)S(1)}, bf16[512,128]{1,0:T(8,128)(2,1)S(1)}, u32[]{:S(2)}, u32[]{:S(2)}) collective-permute-start(bf16[512,128]{1,0:T(8,128)(2,1)S(1)} %bitcast.73), channel_id=1, source_target_pairs={{0,8},{8,16},{16,24},{24,0},{1,9},{9,17},{17,25},{25,1},{2,10},{10... | collective-permute-start | bytes 393224 | tf_op jit(solution)/shard_map/ppermute | solution.py:26
  27.2 14.0 %collective-permute-start = (bf16[512,128]{1,0:T(8,128)(2,1)S(1)}, bf16[512,128]{1,0:T(8,128)(2,1)S(1)}, u32[]{:S(2)}, u32[]{:S(2)}) collective-permute-start(bf16[512,128]{1,0:T(8,128)(2,1)S(1)} %bitcast.74), channel_id=1, source_target_pairs={{0,24},{8,0},{16,8},{24,16},{1,25},{9,1},{17,9},{25,17},{2,26},{10... | collective-permute-start | bytes 393224 | tf_op jit(solution)/shard_map/ppermute | solution.py:26
  29.6 14.6 %collective-permute-start.16 = (bf16[2,512,128]{2,1,0:T(8,128)(2,1)S(1)}, bf16[2,512,128]{2,1,0:T(8,128)(2,1)S(1)}, u32[]{:S(2)}, u32[]{:S(2)}) collective-permute-start(bf16[2,512,128]{2,1,0:T(8,128)(2,1)S(1)} %pad_maximum_fusion.4.refs_12_), channel_id=1, source_target_pairs={{0,8},{8,16},{16,24},{24,0},{1,9},{9,17},{17,25},{25,1},{2,10},{10... | collective-permute-start | bytes 786440 | tf_op jit(solution)/shard_map/ppermute | solution.py:26
  33.3 11.0 %collective-permute-start.6 = (bf16[2,512,128]{2,1,0:T(8,128)(2,1)S(1)}, bf16[2,512,128]{2,1,0:T(8,128)(2,1)S(1)}, u32[]{:S(2)}, u32[]{:S(2)}) collective-permute-start(bf16[2,512,128]{2,1,0:T(8,128)(2,1)S(1)} %pad_maximum_fusion.2.refs_4_), channel_id=1, source_target_pairs={{0,1},{1,0},{4,5},{5,4},{2,3},{3,2},{6,7},{7,6},{8,9},{9,8},{12,13... | collective-permute-start | bytes 786440 | tf_op jit(solution)/shard_map/ppermute | solution.py:30
  33.6 9.6 %collective-permute-start.9 = (bf16[512,128]{1,0:T(8,128)(2,1)S(1)}, bf16[512,128]{1,0:T(8,128)(2,1)S(1)}, u32[]{:S(2)}, u32[]{:S(2)}) collective-permute-start(bf16[512,128]{1,0:T(8,128)(2,1)S(1)} %bitcast.70), channel_id=1, source_target_pairs={{0,1},{1,0},{4,5},{5,4},{2,3},{3,2},{6,7},{7,6},{8,9},{9,8},{12,13... | collective-permute-start | bytes 393224 | tf_op jit(solution)/shard_map/ppermute | solution.py:30
  36.9 49.2 %all-to-all-start.1 = ((bf16[8,256,256]{2,1,0:T(8,128)(2,1)}), bf16[8,256,256]{2,1,0:T(8,128)(2,1)}, u32[]{:S(2)}, u32[]{:S(2)}) async-start(bf16[8,256,256]{2,1,0:T(8,128)(2,1)} %broadcast_in_dim.9), calls=%async_computation.1 | async-start | bytes 2097152 | tf_op jit(solution)/shard_map/all_to_all | solution.py:21
  41.2 5.3 %collective-permute-start.15 = (bf16[2,512,128]{2,1,0:T(8,128)(2,1)S(1)}, bf16[2,512,128]{2,1,0:T(8,128)(2,1)S(1)}, u32[]{:S(2)}, u32[]{:S(2)}) collective-permute-start(bf16[2,512,128]{2,1,0:T(8,128)(2,1)S(1)} %pad_maximum_fusion.4.refs_12_), channel_id=1, source_target_pairs={{0,24},{8,0},{16,8},{24,16},{1,25},{9,1},{17,9},{25,17},{2,26},{10... | collective-permute-start | bytes 786440 | tf_op jit(solution)/shard_map/ppermute | solution.py:26
  41.3 6.5 %collective-permute-start.7 = (bf16[2,512,128]{2,1,0:T(8,128)(2,1)S(1)}, bf16[2,512,128]{2,1,0:T(8,128)(2,1)S(1)}, u32[]{:S(2)}, u32[]{:S(2)}) collective-permute-start(bf16[2,512,128]{2,1,0:T(8,128)(2,1)S(1)} %pad_maximum_fusion.2.refs_4_), channel_id=1, source_target_pairs={{0,5},{5,0},{1,4},{4,1},{2,7},{7,2},{3,6},{6,3},{8,13},{13,8},{9,1... | collective-permute-start | bytes 786440 | tf_op jit(solution)/shard_map/ppermute | solution.py:34
  43.2 9.2 %collective-permute-start.2 = (bf16[2,512,128]{2,1,0:T(8,128)(2,1)S(1)}, bf16[2,512,128]{2,1,0:T(8,128)(2,1)S(1)}, u32[]{:S(2)}, u32[]{:S(2)}) collective-permute-start(bf16[2,512,128]{2,1,0:T(8,128)(2,1)S(1)} %pad_maximum_fusion.1.refs_0_), channel_id=1, source_target_pairs={{0,5},{5,0},{1,4},{4,1},{2,7},{7,2},{3,6},{6,3},{8,13},{13,8},{9,1... | collective-permute-start | bytes 786440 | tf_op jit(solution)/shard_map/ppermute | solution.py:34
  44.2 9.6 %collective-permute-start.1 = (bf16[2,512,128]{2,1,0:T(8,128)(2,1)S(1)}, bf16[2,512,128]{2,1,0:T(8,128)(2,1)S(1)}, u32[]{:S(2)}, u32[]{:S(2)}) collective-permute-start(bf16[2,512,128]{2,1,0:T(8,128)(2,1)S(1)} %pad_maximum_fusion.1.refs_0_), channel_id=1, source_target_pairs={{0,1},{1,0},{4,5},{5,4},{2,3},{3,2},{6,7},{7,6},{8,9},{9,8},{12,13... | collective-permute-start | bytes 786440 | tf_op jit(solution)/shard_map/ppermute | solution.py:30
  44.3 6.3 %collective-permute-start.10 = (bf16[2,512,128]{2,1,0:T(8,128)(2,1)S(1)}, bf16[2,512,128]{2,1,0:T(8,128)(2,1)S(1)}, u32[]{:S(2)}, u32[]{:S(2)}) collective-permute-start(bf16[2,512,128]{2,1,0:T(8,128)(2,1)S(1)} %pad_maximum_fusion.3.refs_8_), channel_id=1, source_target_pairs={{0,24},{8,0},{16,8},{24,16},{1,25},{9,1},{17,9},{25,17},{2,26},{10... | collective-permute-start | bytes 786440 | tf_op jit(solution)/shard_map/ppermute | solution.py:26
  46.5 9.8 %collective-permute-start.12 = (bf16[2,512,128]{2,1,0:T(8,128)(2,1)S(1)}, bf16[2,512,128]{2,1,0:T(8,128)(2,1)S(1)}, u32[]{:S(2)}, u32[]{:S(2)}) collective-permute-start(bf16[2,512,128]{2,1,0:T(8,128)(2,1)S(1)} %pad_maximum_fusion.3.refs_8_), channel_id=1, source_target_pairs={{0,8},{8,16},{16,24},{24,0},{1,9},{9,17},{17,25},{25,1},{2,10},{10... | collective-permute-start | bytes 786440 | tf_op jit(solution)/shard_map/ppermute | solution.py:26
  47.8 8.5 %collective-permute-start.17 = (bf16[2,512,128]{2,1,0:T(8,128)(2,1)S(1)}, bf16[2,512,128]{2,1,0:T(8,128)(2,1)S(1)}, u32[]{:S(2)}, u32[]{:S(2)}) collective-permute-start(bf16[2,512,128]{2,1,0:T(8,128)(2,1)S(1)} %collective-permute-done.16.refs_15_), channel_id=1, source_target_pairs={{0,8},{8,16},{16,24},{24,0},{1,9},{9,17},{17,25},{25,1},{2,10},{10... | collective-permute-start | bytes 786440 | tf_op jit(solution)/shard_map/ppermute | solution.py:26
  50.6 8.8 %collective-permute-start.8 = (bf16[2,512,128]{2,1,0:T(8,128)(2,1)S(1)}, bf16[2,512,128]{2,1,0:T(8,128)(2,1)S(1)}, u32[]{:S(2)}, u32[]{:S(2)}) collective-permute-start(bf16[2,512,128]{2,1,0:T(8,128)(2,1)S(1)} %collective-permute-done.6.refs_5_), channel_id=1, source_target_pairs={{0,5},{5,0},{1,4},{4,1},{2,7},{7,2},{3,6},{6,3},{8,13},{13,8},{9,1... | collective-permute-start | bytes 786440 | tf_op jit(solution)/shard_map/ppermute | solution.py:34
  52.5 7.0 %collective-permute-start.11 = (bf16[2,512,128]{2,1,0:T(8,128)(2,1)S(1)}, bf16[2,512,128]{2,1,0:T(8,128)(2,1)S(1)}, u32[]{:S(2)}, u32[]{:S(2)}) collective-permute-start(bf16[2,512,128]{2,1,0:T(8,128)(2,1)S(1)} %collective-permute-done.10.refs_9_), channel_id=1, source_target_pairs={{0,24},{8,0},{16,8},{24,16},{1,25},{9,1},{17,9},{25,17},{2,26},{10... | collective-permute-start | bytes 786440 | tf_op jit(solution)/shard_map/ppermute | solution.py:26
  53.8 5.6 %collective-permute-start.3 = (bf16[2,512,128]{2,1,0:T(8,128)(2,1)S(1)}, bf16[2,512,128]{2,1,0:T(8,128)(2,1)S(1)}, u32[]{:S(2)}, u32[]{:S(2)}) collective-permute-start(bf16[2,512,128]{2,1,0:T(8,128)(2,1)S(1)} %collective-permute-done.2.refs_2_), channel_id=1, source_target_pairs={{0,1},{1,0},{4,5},{5,4},{2,3},{3,2},{6,7},{7,6},{8,9},{9,8},{12,13... | collective-permute-start | bytes 786440 | tf_op jit(solution)/shard_map/ppermute | solution.py:30
  56.2 29.6 %copy-start.4 = (bf16[256,1024]{1,0:T(8,128)(2,1)S(1)}, bf16[256,1024]{1,0:T(8,128)(2,1)}, u32[]{:S(2)}) copy-start(bf16[256,1024]{1,0:T(8,128)(2,1)} %param.7) | copy-start | bytes 1572868
  71.0 2.0 %copy-start.1 = (bf16[4,2048,256]{2,1,0:T(8,128)(2,1)}, bf16[4,2048,256]{2,1,0:T(8,128)(2,1)S(1)}, u32[]{:S(2)}) copy-start(bf16[4,2048,256]{2,1,0:T(8,128)(2,1)S(1)} %get-tuple-element.13) | copy-start | bytes 12582916
  72.9 1.4 copy-start.2
  74.3 11.5 %collective-permute-start.18 = (f32[256,1024]{1,0:T(8,128)S(1)}, f32[256,1024]{1,0:T(8,128)S(1)}, u32[]{:S(2)}, u32[]{:S(2)}) collective-permute-start(f32[256,1024]{1,0:T(8,128)S(1)} %get-tuple-element.10), channel_id=1, source_target_pairs={{0,2},{2,0},{1,3},{3,1},{4,6},{6,4},{5,7},{7,5},{8,10},{10,8},{9,1... | collective-permute-start | bytes 3145736 | tf_op jit(solution)/shard_map/ppermute | solution.py:56
  85.8 3.1 %copy-start.3 = (bf16[1024,1024]{1,0:T(8,128)(2,1)S(1)}, bf16[1024,1024]{1,0:T(8,128)(2,1)}, u32[]{:S(2)}) copy-start(bf16[1024,1024]{1,0:T(8,128)(2,1)} %copy-done.2) | copy-start | bytes 6291460
  86.1 2.8 %collective-permute-start.19 = (bf16[256,1024]{1,0:T(8,128)(2,1)S(1)}, bf16[256,1024]{1,0:T(8,128)(2,1)S(1)}, u32[]{:S(2)}, u32[]{:S(2)}) collective-permute-start(bf16[256,1024]{1,0:T(8,128)(2,1)S(1)} %multiply_convert_fusion), channel_id=1, source_target_pairs={{0,2},{2,0},{1,3},{3,1},{4,6},{6,4},{5,7},{7,5},{8,10},{10,8},{9,1... | collective-permute-start | bytes 1572872 | tf_op jit(solution)/shard_map/ppermute | solution.py:56
  90.9 36.1 %all-to-all-start.2 = ((bf16[8,2,16,8,256]{4,3,2,1,0:T(8,128)(2,1)}), bf16[8,2,16,8,256]{4,3,2,1,0:T(8,128)(2,1)S(1)}, u32[]{:S(2)}, u32[]{:S(2)}) async-start(bf16[8,2,16,8,256]{4,3,2,1,0:T(8,128)(2,1)} %pad_maximum_fusion), calls=%async_computation.2 | async-start | bytes 2097152 | tf_op jit(solution)/shard_map/all_to_all | solution.py:180
  97.8 31.2 %collective-permute-start.20 = (bf16[2048,256]{1,0:T(8,128)(2,1)}, bf16[2048,256]{1,0:T(8,128)(2,1)S(1)}, u32[]{:S(2)}, u32[]{:S(2)}) collective-permute-start(bf16[2048,256]{1,0:T(8,128)(2,1)} %bitcast.10), channel_id=1, source_target_pairs={{0,2},{2,0},{1,3},{3,1},{4,6},{6,4},{5,7},{7,5},{8,10},{10,8},{9,1... | collective-permute-start | bytes 3145736 | tf_op jit(solution)/shard_map/ppermute | solution.py:56
  144.5 2.9 %collective-permute-start.21 = (f32[8,2048]{1,0:T(8,128)S(1)}, f32[8,2048]{1,0:T(8,128)S(1)}, u32[]{:S(2)}, u32[]{:S(2)}) collective-permute-start(f32[8,2048]{1,0:T(8,128)S(1)} %get-tuple-element.23), channel_id=1, source_target_pairs={{0,2},{2,0},{1,3},{3,1},{4,6},{6,4},{5,7},{7,5},{8,10},{10,8},{9,1... | collective-permute-start | bytes 196616 | tf_op jit(solution)/shard_map/ppermute | solution.py:56
where the time goes:
time: 164 us
  blocking collectives  46.1 us (28%)
  starting transfers between devices  44.2 us (27%)
  waiting for transfers between devices  40.4 us (25%)
  Pallas kernels  11.5 us (7%)
  local copies, waits for them, and re-layouts  9.17 us (6%)
  matrix products  8.12 us (5%)
  other arithmetic  3.08 us (2%)
    all_to_all x1, waiting for transfers between devices, body(): parts = lax.all_to_all(partial, 'grid', 0, 0, tiled=True)  28.7 us
    all_to_all x1, blocking collectives, sent_to_all(): return lax.all_to_all(copies, axis, split_axis=0, concat_axis=0, tiled=True)  19.3 us
    all_to_all x1, blocking collectives, body(): lax.all_to_all(terms.reshape(-1, share, nrows), CHIPS, 0, 0, tiled=True)  14.9 us
    ppermute x4, starting transfers between devices, other_core(): return lax.ppermute(x, 'core', [(0, 1), (1, 0)])  12.2 us
    all_to_all x1, blocking collectives, body(): both = lax.all_to_all(both, ('grid', 'core'), 0, 0, tiled=True)  11.9 us
    pallas_call x1, Pallas kernels, pick(): pl.pallas_call(pick_kernel, grid=(4,), in_specs=[pl.BlockSpec((total, nro...  11.5 us
    ppermute x9, starting transfers between devices, from_next(): return lax.ppermute(x, 'y', [(i, (i - step) % n) for i in range(n)])  10.2 us
    ppermute x4, starting transfers between devices, with_mirror(): return lax.ppermute(x, X, [(0, 3), (3, 0), (1, 2), (2, 1)])  7.23 us
  transfers between devices with their start and end apart: 24, of which 8 were waited for; matrix products, arithmetic and copies ran while one was open for 6% of the time, Pallas kernels for 7%

commit v1 on v0

--- a/solution.py
+++ b/solution.py
@@ -56,72 +56,91 @@
     return lax.ppermute(x, "core", [(0, 1), (1, 0)])
 
 
-def pick_kernel(choose_ref, *refs):
-    pieces, outs = refs[:-4], refs[-4:]
-    own_ref, other_ref, picked_ref, columns_ref = outs
-    step = pl.program_id(0)
+def pick_kernel(spots_ref, *refs):
+    pieces, outs = refs[:16], refs[16:20]
+    own_ref, other_ref, picked_ref, columns_out_ref = outs
+    wide_ref, chosen_ref, rows_ref, columns_ref, sem = refs[20:]
     rows = own_ref.shape[0]
+    rest = picked_ref.shape[0]
     height, width = pieces[0].shape[1:]
     alpha, beta = pieces[:8], pieces[8:]
-
-    @pl.when(step == 0)
-    def _():
-        own_ref[...] = jnp.zeros_like(own_ref)
-        other_ref[...] = jnp.zeros_like(other_ref)
+    group = 256
 
     for at in range(4):
-
-        @pl.when(step == at)
-        def _():
-            for col, roles in enumerate(((0, 1), (3, 2))):
-                for k, role in enumerate(roles):
-                    for part, piece in enumerate(
-                        (alpha[role + 4 * (at // 2)][at % 2], beta[at + 4 * (role // 2)][role % 2])
-                    ):
-                        top = (2 * k + part) * height
-                        columns_ref[0, top : top + height, col * width : (col + 1) * width] = piece
-
-    picked = jnp.dot(choose_ref[...], columns_ref[0], preferred_element_type=F32).astype(BF)
-    picked_ref[...] = picked[2 * rows :]
+        for col, roles in enumerate(((0, 1), (3, 2))):
+            for k, role in enumerate(roles):
+                for part, (piece, which) in enumerate(
+                    ((alpha[role + 4 * (at // 2)], at % 2), (beta[at + 4 * (role // 2)], role % 2))
+                ):
+                    top = (2 * k + part) * height
+
+                    def spread(i, _, piece=piece, which=which, top=top, at=at, col=col):
+                        start = pl.multiple_of(i * group, group)
+                        block = piece[which, pl.ds(start, group), :]
+                        columns_ref[at, pl.ds(top + start, group), col * width : (col + 1) * width] = block
+                        wide_ref[pl.ds((top + start) * 8 + 2 * at + col, group, stride=8), :] = block.astype(F32)
+                        return _
+
+                    lax.fori_loop(0, height // group, spread, 0)
+
+    keep = pltpu.make_async_copy(columns_ref, columns_out_ref, sem)
+    keep.start()
+
+    def choose(i, _):
+        for k in range(16):
+            spot = pl.multiple_of(spots_ref[i * 16 + k] * 8, 8)
+            to = pl.multiple_of(i * 128 + k * 8, 8)
+            chosen_ref[pl.ds(to, 8), :] = wide_ref[pl.ds(spot, 8), :]
+        return _
+
+    lax.fori_loop(0, (2 * rows + rest) // 16, choose, 0)
+
+    for target, first, count in ((rows_ref, 0, 2 * rows), (picked_ref, 2 * rows, rest)):
+        for k in range(8):
+
+            def gather(i, _, target=target, first=first, k=k):
+                start = pl.multiple_of(i * group, group)
+                block = chosen_ref[pl.ds((first + start) * 8 + k, group, stride=8), :]
+                target[pl.ds(start, group), k * width : (k + 1) * width] = block.astype(BF)
+                return _
+
+            lax.fori_loop(0, count // group, gather, 0)
+
     for k, out in enumerate((own_ref, other_ref)):
-        out[...] += lax.dot_general(
-            picked[k * rows : (k + 1) * rows],
-            picked[2 * rows :],
-            (((1,), (1,)), ((), ())),
-            preferred_element_type=F32,
-        )
-
-
-def pick(choose, pieces, rows):
+        out[...] = lax.dot_general(
+            rows_ref[k * rows : (k + 1) * rows], picked_ref[...], (((1,), (1,)), ((), ())),
+            preferred_element_type=F32)
+    keep.wait()
+
+
+def pick(spots, pieces, rows):
     _, height, width = pieces[0].shape
-    total, nrows = choose.shape
+    total, nrows = spots.shape[0], 4 * height
     rest = total - 2 * rows
-    whole = lambda i: (0, 0)
+    vm = pl.BlockSpec(memory_space=pltpu.VMEM)
     return pl.pallas_call(
         pick_kernel,
-        grid=(4,),
-        in_specs=[pl.BlockSpec((total, nrows), whole)]
-        + [pl.BlockSpec((2, height, width), lambda i: (0, 0, 0))] * len(pieces),
-        out_specs=[
-            pl.BlockSpec((rows, rest), whole),
-            pl.BlockSpec((rows, rest), whole),
-            pl.BlockSpec((rest, 2 * width), lambda i: (0, i)),
-            pl.BlockSpec((1, nrows, 2 * width), lambda i: (i, 0, 0)),
-        ],
+        in_specs=[pl.BlockSpec(memory_space=pltpu.SMEM)] + [vm] * 16,
+        out_specs=[vm] * 3 + [pl.BlockSpec(memory_space=pltpu.HBM)],
         out_shape=[
             jax.ShapeDtypeStruct((rows, rest), F32),
             jax.ShapeDtypeStruct((rows, rest), F32),
             jax.ShapeDtypeStruct((rest, 8 * width), BF),
-            jax.ShapeDtypeStruct((4, nrows, 2 * width), BF),
+            pltpu.HBM((4, nrows, 2 * width), BF),
         ],
-        compiler_params=pltpu.CompilerParams(dimension_semantics=("arbitrary",), vmem_limit_bytes=30 << 20),
+        scratch_shapes=[
+            pltpu.VMEM((nrows * 8, width), F32),
+            pltpu.VMEM((total * 8, width), F32),
+            pltpu.VMEM((2 * rows, 8 * width), BF),
+            pltpu.VMEM((4, nrows, 2 * width), BF),
+            pltpu.SemaphoreType.DMA,
+        ],
+        compiler_params=pltpu.CompilerParams(vmem_limit_bytes=26 << 20),
         cost_estimate=pl.CostEstimate(
-            flops=16 * width * (total * nrows + 2 * rows * rest),
-            bytes_accessed=16 * nrows * width,
-            transcendentals=0,
+            flops=4 * rows * rest * 8 * width, bytes_accessed=32 * nrows * width, transcendentals=0
         ),
         name="pick",
-    )(choose, *pieces)
+    )(spots, *pieces)
 
 
 def body(orbitals, points, fitting, screened):
@@ -149,20 +168,18 @@
     b_first, b_second = jnp.stack(betas[:2]), jnp.stack(betas[2:])
     pieces = [x for part in along_x(a_first, a_second) + along_y(b_first, b_second) for x in part]
 
-    fit_own = sent_to_all(fitting, "grid").reshape(nrows, row_block)
+    copies = jnp.broadcast_to(fitting, (n_grid, *fitting.shape))
+    fit_own = lax.all_to_all(copies, "grid", 0, 0, tiled=True).reshape(nrows, row_block)
     fit_other = other_core(fit_own)
 
-    near = lax.broadcasted_iota(jnp.int32, (nrows,), 0)
-    half_of = lax.rem(near // (nrows // 2) + pts, 2)
-    within = lax.rem(near, nrows // 2)
-    ids = (within // part) * rows_dev + half_of * part + lax.rem(within, part)
     mine = lax.dynamic_slice_in_dim(points, plane_index * row_block, row_block, 0)
     theirs_index = plane_index + (1 - 2 * core) * lax.axis_size("pts")
     theirs = lax.dynamic_slice_in_dim(points, theirs_index * row_block, row_block, 0)
     block = lax.dynamic_slice_in_dim(points, grid_index * column_block, column_block, 0)
     wanted = jnp.concatenate([mine, theirs, block])
-    choose = (wanted[:, None] == ids[None]).astype(BF)
-    density, density_other, picked, columns = pick(choose, pieces, row_block)
+    half_of = lax.rem(wanted, rows_dev) // part
+    spots = (half_of ^ pts) * (nrows // 2) + wanted // rows_dev * part + lax.rem(wanted, part)
+    density, density_other, picked, columns = pick(spots, pieces, row_block)
 
     density = density + other_core(density_other)
     masked = (density * screened.astype(F32)).astype(BF)

time: 164 us -> 156 us (0.951)
  local copies, waits for them, and re-layouts: 9.17 us -> 6.29 us
  Pallas kernels: 11.5 us -> 9.02 us
    ppermute x4, waiting for transfers between devices: 3.45 us -> 0.24 us  [with_mirror(): return lax.ppermute(x, X, [(0, 3), (3, 0), (1, 2), (2, 1)])]
    pallas_call x1, Pallas kernels: 11.5 us -> 9.02 us  [pick(): pl.pallas_call(pick_kernel, in_specs=[pl.BlockSpec(memory_space=pltpu.SME...]
    broadcast_in_dim x2 -> x1, local copies, waits for them, and re-layouts: 2.09 us -> 0.04 us  [sent_to_all(): copies = jnp.broadcast_to(x, (lax.axis_size(axis), *x.shape))]
    unnamed x10, local copies, waits for them, and re-layouts: 4.17 us -> 2.21 us
  transfers between devices with their start and end apart: 24 -> 24, of which waited for: 8 -> 10; matrix products, arithmetic and copies ran while one was open for 6% -> 4% of each run, Pallas kernels for 7% -> 6%
where the time goes in v1:
time: 156 us
  blocking collectives  46.1 us (30%)
  starting transfers between devices  43.4 us (28%)
  waiting for transfers between devices  41.3 us (26%)
  Pallas kernels  9.02 us (6%)
  matrix products  6.53 us (4%)
  local copies, waits for them, and re-layouts  6.29 us (4%)
  other arithmetic  2 us (1%)
    all_to_all x1, waiting for transfers between devices, body(): parts = lax.all_to_all(partial, 'grid', 0, 0, tiled=True)  28.6 us
    all_to_all x1, blocking collectives, sent_to_all(): return lax.all_to_all(copies, axis, split_axis=0, concat_axis=0, tiled=True)  19.3 us
    all_to_all x1, blocking collectives, body(): lax.all_to_all(terms.reshape(-1, share, nrows), CHIPS, 0, 0, tiled=True)  14.9 us
    ppermute x4, starting transfers between devices, other_core(): return lax.ppermute(x, 'core', [(0, 1), (1, 0)])  12.9 us
    all_to_all x1, blocking collectives, body(): both = lax.all_to_all(both, ('grid', 'core'), 0, 0, tiled=True)  11.9 us
    ppermute x9, starting transfers between devices, from_next(): return lax.ppermute(x, 'y', [(i, (i - step) % n) for i in range(n)])  9.15 us
    pallas_call x1, Pallas kernels, pick(): pl.pallas_call(pick_kernel, in_specs=[pl.BlockSpec(memory_space=pltpu.SME...  9.02 us
    ppermute x4, starting transfers between devices, with_mirror(): return lax.ppermute(x, X, [(0, 3), (3, 0), (1, 2), (2, 1)])  8.44 us
  transfers between devices with their start and end apart: 24, of which 10 were waited for; matrix products, arithmetic and copies ran while one was open for 4% of the time, Pallas kernels for 6%

profile of v1, /device:TPU:1, one launch (start us, length us, event | category | flops | bytes accessed | tf_op | source)
XLA Modules:
  0.0 155.7 jit_solution(7375734494475601497)
XLA Ops:
  0.6 0.0 copy-start
  0.7 0.8 copy-done
  1.5 19.3 %all_to_all.25 = bf16[8,128,128]{2,1,0:T(8,128)(2,1)S(1)} all-to-all(bf16[8,128,128]{2,1,0:T(8,128)(2,1)S(1)} %broadcast_in_dim.6), channel_id=1, replica_groups=mesh['grid'=8,'y'=4,'xh'=2,'core'=2,'pts'=2] {'grid'}, dimensions={0} | all-to-all | bytes 524288 | tf_op jit(solution)/shard_map/all_to_all | solution.py:21
  20.8 2.6 %collective-permute-start.13 = (bf16[512,128]{1,0:T(8,128)(2,1)S(1)}, bf16[512,128]{1,0:T(8,128)(2,1)S(1)}, u32[]{:S(2)}, u32[]{:S(2)}) collective-permute-start(bf16[512,128]{1,0:T(8,128)(2,1)S(1)} %bitcast.72), channel_id=1, source_target_pairs={{0,5},{5,0},{1,4},{4,1},{2,7},{7,2},{3,6},{6,3},{8,13},{13,8},{9,1... | collective-permute-start | bytes 393224 | tf_op jit(solution)/shard_map/ppermute | solution.py:34
  23.4 0.5 collective-permute-start.14
  23.9 2.9 %collective-permute-start.4 = (bf16[512,128]{1,0:T(8,128)(2,1)S(1)}, bf16[512,128]{1,0:T(8,128)(2,1)S(1)}, u32[]{:S(2)}, u32[]{:S(2)}) collective-permute-start(bf16[512,128]{1,0:T(8,128)(2,1)S(1)} %bitcast.68), channel_id=1, source_target_pairs={{0,16},{8,24},{16,0},{24,8},{1,17},{9,25},{17,1},{25,9},{2,18},{10... | collective-permute-start | bytes 393224 | tf_op jit(solution)/shard_map/ppermute | solution.py:26
  26.8 0.4 collective-permute-start.5
  27.2 0.3 collective-permute-start.9
  27.5 1.3 collective-permute-done.14
  28.9 1.4 collective-permute-start.16
  30.2 3.0 %collective-permute-done.5 = bf16[512,128]{1,0:T(8,128)(2,1)S(1)} collective-permute-done((bf16[512,128]{1,0:T(8,128)(2,1)S(1)}, bf16[512,128]{1,0:T(8,128)(2,1)S(1)}, u32[]{:S(2)}, u32[]{:S(2)}) %collective-permute-start.5) | collective-permute-done | bytes 131104 | tf_op jit(solution)/shard_map/ppermute | solution.py:26
  33.3 0.3 collective-permute-start.6
  33.6 0.0 collective-permute-start
  33.6 0.0 collective-permute-start.15
  33.7 2.5 %collective-permute-start.7 = (bf16[2,512,128]{2,1,0:T(8,128)(2,1)S(1)}, bf16[2,512,128]{2,1,0:T(8,128)(2,1)S(1)}, u32[]{:S(2)}, u32[]{:S(2)}) collective-permute-start(bf16[2,512,128]{2,1,0:T(8,128)(2,1)S(1)} %pad_maximum_fusion.2.refs_4_), channel_id=1, source_target_pairs={{0,5},{5,0},{1,4},{4,1},{2,7},{7,2},{3,6},{6,3},{8,13},{13,8},{9,1... | collective-permute-start | bytes 786440 | tf_op jit(solution)/shard_map/ppermute | solution.py:34
  36.3 1.2 collective-permute-done
  37.5 1.2 collective-permute-start.10
  38.7 0.0 collective-permute-done.16.refs_15_
  38.7 2.6 %collective-permute-start.2 = (bf16[2,512,128]{2,1,0:T(8,128)(2,1)S(1)}, bf16[2,512,128]{2,1,0:T(8,128)(2,1)S(1)}, u32[]{:S(2)}, u32[]{:S(2)}) collective-permute-start(bf16[2,512,128]{2,1,0:T(8,128)(2,1)S(1)} %pad_maximum_fusion.1.refs_0_), channel_id=1, source_target_pairs={{0,5},{5,0},{1,4},{4,1},{2,7},{7,2},{3,6},{6,3},{8,13},{13,8},{9,1... | collective-permute-start | bytes 786440 | tf_op jit(solution)/shard_map/ppermute | solution.py:34
  41.3 0.0 collective-permute-done.6.refs_5_
  41.3 0.5 collective-permute-start.12
  41.8 1.1 broadcast_in_dim.7
  43.0 4.2 %all-to-all-start.1 = ((bf16[8,256,256]{2,1,0:T(8,128)(2,1)}), bf16[8,256,256]{2,1,0:T(8,128)(2,1)}, u32[]{:S(2)}, u32[]{:S(2)}) async-start(bf16[8,256,256]{2,1,0:T(8,128)(2,1)} %broadcast_in_dim.7), calls=%async_computation.1 | async-start | bytes 2097152 | tf_op jit(solution)/shard_map/all_to_all | solution.py:172
  47.2 0.0 collective-permute-done.15.refs_13_
  47.2 0.1 collective-permute-start.1
  47.4 0.1 collective-permute-start.17
  47.5 0.8 collective-permute-start.8
  48.2 2.6 %collective-permute-start.11 = (bf16[2,512,128]{2,1,0:T(8,128)(2,1)S(1)}, bf16[2,512,128]{2,1,0:T(8,128)(2,1)}, u32[]{:S(2)}, u32[]{:S(2)}) collective-permute-start(bf16[2,512,128]{2,1,0:T(8,128)(2,1)S(1)} %collective-permute-done.10.refs_9_), channel_id=1, source_target_pairs={{0,24},{8,0},{16,8},{24,16},{1,25},{9,1},{17,9},{25,17},{2,26},{10... | collective-permute-start | bytes 786440 | tf_op jit(solution)/shard_map/ppermute | solution.py:26
  50.8 0.7 collective-permute-start.3
  51.6 0.7 dynamic_slice.24
  52.3 0.8 fusion.18
  53.1 0.0 copy-start.3
  53.2 2.3 %collective-permute-done.17.refs_14_ = bf16[2,512,128]{2,1,0:T(8,128)(2,1)S(1)} collective-permute-done((bf16[2,512,128]{2,1,0:T(8,128)(2,1)S(1)}, bf16[2,512,128]{2,1,0:T(8,128)(2,1)S(1)}, u32[]{:S(2)}, u32[]{:S(2)}) %collective-permute-start.17) | collective-permute-done | bytes 262176 | tf_op jit(solution)/shard_map/ppermute | solution.py:26
  55.5 0.2 collective-permute-done.8.refs_7_
  55.7 0.6 collective-permute-done.3.refs_3_
  56.3 9.0 %pick.1 = (f32[256,1024]{1,0:T(8,128)S(1)}, f32[256,1024]{1,0:T(8,128)S(1)}, bf16[1024,1024]{1,0:T(8,128)(2,1)S(1)}, bf16[4,2048,256]{2,1,0:T(8,128)(2,1)}) custom-call(s32[1536]{0:T(1024)S(1)} %fusion.10.spots_ref, bf16[2,512,128]{2,1,0:T(8,128)(2,1)S(1)} %pad_maximum_fusion.1.refs_0_, bf16[2,512,128]{2,1,0:T(8,128)(2,1)S(1)} %collective-permute-done.1.refs_1_, ...), custom_call_target="tpu_custom_call" | custom-call | flops 1073741824 | bytes 8388608 | tf_op jit(solution)/shard_map/pick/pallas_call | solution.py:121
  65.4 1.4 copy-done.1
  66.8 9.8 %collective-permute-start.18 = (f32[256,1024]{1,0:T(8,128)S(1)}, f32[256,1024]{1,0:T(8,128)S(1)}, u32[]{:S(2)}, u32[]{:S(2)}) collective-permute-start(f32[256,1024]{1,0:T(8,128)S(1)} %get-tuple-element.10), channel_id=1, source_target_pairs={{0,2},{2,0},{1,3},{3,1},{4,6},{6,4},{5,7},{7,5},{8,10},{10,8},{9,1... | collective-permute-start | bytes 3145736 | tf_op jit(solution)/shard_map/ppermute | solution.py:56
  76.5 2.3 %collective-permute-done.18 = f32[256,1024]{1,0:T(8,128)S(1)} collective-permute-done((f32[256,1024]{1,0:T(8,128)S(1)}, f32[256,1024]{1,0:T(8,128)S(1)}, u32[]{:S(2)}, u32[]{:S(2)}) %collective-permute-start.18) | collective-permute-done | bytes 1048608 | tf_op jit(solution)/shard_map/ppermute | solution.py:56
  78.8 0.3 multiply_convert_fusion
  79.1 0.5 collective-permute-start.19
  79.6 0.8 convolution_convert_fusion.1
  80.3 0.8 collective-permute-done.19
  81.1 0.8 convolution_convert_fusion
  81.9 0.1 copy_bitcast_fusion
  82.0 1.1 pad_maximum_fusion
  83.1 6.7 %all-to-all-start.2 = ((bf16[8,2,16,8,256]{4,3,2,1,0:T(8,128)(2,1)}), bf16[8,2,16,8,256]{4,3,2,1,0:T(8,128)(2,1)S(1)}, u32[]{:S(2)}, u32[]{:S(2)}) async-start(bf16[8,2,16,8,256]{4,3,2,1,0:T(8,128)(2,1)} %pad_maximum_fusion), calls=%async_computation.2 | async-start | bytes 2097152 | tf_op jit(solution)/shard_map/all_to_all | solution.py:197
  89.8 0.7 collective-permute-start.20
  90.5 28.6 %all-to-all-done.2 = bf16[8,2,16,8,256]{4,3,2,1,0:T(8,128)(2,1)S(1)} async-done(((bf16[8,2,16,8,256]{4,3,2,1,0:T(8,128)(2,1)}), bf16[8,2,16,8,256]{4,3,2,1,0:T(8,128)(2,1)S(1)}, u32[]{:S(2)}, u32[]{:S(2)}) %all-to-all-start.2) | async-done | bytes 1048608 | tf_op jit(solution)/shard_map/all_to_all | solution.py:197
  119.1 0.1 reduce_sum.21
  119.2 0.1 fusion.3
  119.3 1.7 %fusion.19 = f32[128,2048]{1,0:T(8,128)S(1)} fusion(bf16[128,256]{1,0:T(8,128)(2,1)S(1)} %bitcast.76, bf16[2048,256]{1,0:T(8,128)(2,1)} %bitcast.10), kind=kOutput, calls=%fused_computation.60 | convolution fusion | flops 134217728 | bytes 2162688 | tf_op jit(solution)/shard_map/dot_general | solution.py:205
  121.1 0.5 fusion.1
  121.5 14.9 %all_to_all.26 = bf16[16,8,2048]{2,1,0:T(8,128)(2,1)S(1)} all-to-all(bf16[16,8,2048]{2,1,0:T(8,128)(2,1)S(1)} %fusion.1), channel_id=1, replica_groups=mesh['grid'=8,'y'=4,'xh'=2,'core'=2,'pts'=2] {'y','xh','pts'}, dimensions={0} | all-to-all | bytes 1048576 | tf_op jit(solution)/shard_map/all_to_all | solution.py:208
  136.4 0.1 convert_reduce_fusion
  136.5 2.0 %collective-permute-start.21 = (f32[8,2048]{1,0:T(8,128)S(1)}, f32[8,2048]{1,0:T(8,128)S(1)}, u32[]{:S(2)}, u32[]{:S(2)}) collective-permute-start(f32[8,2048]{1,0:T(8,128)S(1)} %get-tuple-element.23), channel_id=1, source_target_pairs={{0,2},{2,0},{1,3},{3,1},{4,6},{6,4},{5,7},{7,5},{8,10},{10,8},{9,1... | collective-permute-start | bytes 196616 | tf_op jit(solution)/shard_map/ppermute | solution.py:56
  138.5 0.9 collective-permute-done.21
  139.5 0.3 rev.14
  139.8 0.1 fusion.4
  139.9 2.8 %fusion.2 = f32[4,2,2,8,128]{4,3,2,1,0:T(8,128)S(1)} fusion(bf16[16,2048,1]{1,0,2:T(8,128)(2,1)S(1)} %reshape.72, bf16[4,2048,256]{2,1,0:T(8,128)(2,1)} %get-tuple-element.13), kind=kOutput, calls=%fused_computation.6 | convolution fusion | flops 67125248 | bytes 4325376 | tf_op jit(solution)/shard_map/dot_general | solution.py:216
  142.8 0.1 reshape.67
  142.9 0.1 constant_dynamic-slice_fusion
  143.1 11.9 %all_to_all.27 = f32[16,2,8,128]{3,2,1,0:T(8,128)S(1)} all-to-all(f32[16,2,8,128]{3,2,1,0:T(8,128)S(1)} %copy.17), channel_id=1, replica_groups=mesh['grid'=8,'y'=4,'xh'=2,'core'=2,'pts'=2] {'grid','core'}, dimensions={0} | all-to-all | bytes 262144 | tf_op jit(solution)/shard_map/all_to_all | solution.py:227
  155.0 0.7 slice_bitcast_fusion
  (39 shorter events, 0.5 us)
Async XLA Ops:
  0.6 0.8 copy-start
  0.6 41.2 %copy-start.4 = (bf16[256,256]{1,0:T(8,128)(2,1)S(1)}, bf16[256,256]{1,0:T(8,128)(2,1)}, u32[]{:S(2)}) copy-start(bf16[256,256]{1,0:T(8,128)(2,1)} %param.6) | copy-start | bytes 393220
  20.8 6.7 %collective-permute-start.13 = (bf16[512,128]{1,0:T(8,128)(2,1)S(1)}, bf16[512,128]{1,0:T(8,128)(2,1)S(1)}, u32[]{:S(2)}, u32[]{:S(2)}) collective-permute-start(bf16[512,128]{1,0:T(8,128)(2,1)S(1)} %bitcast.72), channel_id=1, source_target_pairs={{0,5},{5,0},{1,4},{4,1},{2,7},{7,2},{3,6},{6,3},{8,13},{13,8},{9,1... | collective-permute-start | bytes 393224 | tf_op jit(solution)/shard_map/ppermute | solution.py:34
  23.4 5.4 %collective-permute-start.14 = (bf16[512,128]{1,0:T(8,128)(2,1)S(1)}, bf16[512,128]{1,0:T(8,128)(2,1)S(1)}, u32[]{:S(2)}, u32[]{:S(2)}) collective-permute-start(bf16[512,128]{1,0:T(8,128)(2,1)S(1)} %bitcast.73), channel_id=1, source_target_pairs={{0,4},{4,0},{1,5},{5,1},{2,6},{6,2},{3,7},{7,3},{8,12},{12,8},{9,1... | collective-permute-start | bytes 393224 | tf_op jit(solution)/shard_map/ppermute | solution.py:38
  23.9 6.3 %collective-permute-start.4 = (bf16[512,128]{1,0:T(8,128)(2,1)S(1)}, bf16[512,128]{1,0:T(8,128)(2,1)S(1)}, u32[]{:S(2)}, u32[]{:S(2)}) collective-permute-start(bf16[512,128]{1,0:T(8,128)(2,1)S(1)} %bitcast.68), channel_id=1, source_target_pairs={{0,16},{8,24},{16,0},{24,8},{1,17},{9,25},{17,1},{25,9},{2,18},{10... | collective-permute-start | bytes 393224 | tf_op jit(solution)/shard_map/ppermute | solution.py:26
  26.8 6.4 %collective-permute-start.5 = (bf16[512,128]{1,0:T(8,128)(2,1)S(1)}, bf16[512,128]{1,0:T(8,128)(2,1)S(1)}, u32[]{:S(2)}, u32[]{:S(2)}) collective-permute-start(bf16[512,128]{1,0:T(8,128)(2,1)S(1)} %bitcast.69), channel_id=1, source_target_pairs={{0,8},{8,16},{16,24},{24,0},{1,9},{9,17},{17,25},{25,1},{2,10},{10... | collective-permute-start | bytes 393224 | tf_op jit(solution)/shard_map/ppermute | solution.py:26
  27.2 6.5 %collective-permute-start.9 = (bf16[512,128]{1,0:T(8,128)(2,1)S(1)}, bf16[512,128]{1,0:T(8,128)(2,1)S(1)}, u32[]{:S(2)}, u32[]{:S(2)}) collective-permute-start(bf16[512,128]{1,0:T(8,128)(2,1)S(1)} %bitcast.74), channel_id=1, source_target_pairs={{0,1},{1,0},{4,5},{5,4},{2,3},{3,2},{6,7},{7,6},{8,9},{9,8},{12,13... | collective-permute-start | bytes 393224 | tf_op jit(solution)/shard_map/ppermute | solution.py:30
  28.9 9.9 %collective-permute-start.16 = (bf16[2,512,128]{2,1,0:T(8,128)(2,1)S(1)}, bf16[2,512,128]{2,1,0:T(8,128)(2,1)S(1)}, u32[]{:S(2)}, u32[]{:S(2)}) collective-permute-start(bf16[2,512,128]{2,1,0:T(8,128)(2,1)S(1)} %pad_maximum_fusion.4.refs_12_), channel_id=1, source_target_pairs={{0,8},{8,16},{16,24},{24,0},{1,9},{9,17},{17,25},{25,1},{2,10},{10... | collective-permute-start | bytes 786440 | tf_op jit(solution)/shard_map/ppermute | solution.py:26
  33.3 8.0 %collective-permute-start.6 = (bf16[2,512,128]{2,1,0:T(8,128)(2,1)S(1)}, bf16[2,512,128]{2,1,0:T(8,128)(2,1)S(1)}, u32[]{:S(2)}, u32[]{:S(2)}) collective-permute-start(bf16[2,512,128]{2,1,0:T(8,128)(2,1)S(1)} %pad_maximum_fusion.2.refs_4_), channel_id=1, source_target_pairs={{0,1},{1,0},{4,5},{5,4},{2,3},{3,2},{6,7},{7,6},{8,9},{9,8},{12,13... | collective-permute-start | bytes 786440 | tf_op jit(solution)/shard_map/ppermute | solution.py:30
  33.6 3.8 %collective-permute-start = (bf16[512,128]{1,0:T(8,128)(2,1)S(1)}, bf16[512,128]{1,0:T(8,128)(2,1)S(1)}, u32[]{:S(2)}, u32[]{:S(2)}) collective-permute-start(bf16[512,128]{1,0:T(8,128)(2,1)S(1)} %bitcast.70), channel_id=1, source_target_pairs={{0,24},{8,0},{16,8},{24,16},{1,25},{9,1},{17,9},{25,17},{2,26},{10... | collective-permute-start | bytes 393224 | tf_op jit(solution)/shard_map/ppermute | solution.py:26
  33.6 13.6 %collective-permute-start.15 = (bf16[2,512,128]{2,1,0:T(8,128)(2,1)S(1)}, bf16[2,512,128]{2,1,0:T(8,128)(2,1)S(1)}, u32[]{:S(2)}, u32[]{:S(2)}) collective-permute-start(bf16[2,512,128]{2,1,0:T(8,128)(2,1)S(1)} %pad_maximum_fusion.4.refs_12_), channel_id=1, source_target_pairs={{0,24},{8,0},{16,8},{24,16},{1,25},{9,1},{17,9},{25,17},{2,26},{10... | collective-permute-start | bytes 786440 | tf_op jit(solution)/shard_map/ppermute | solution.py:26
  33.7 13.7 %collective-permute-start.7 = (bf16[2,512,128]{2,1,0:T(8,128)(2,1)S(1)}, bf16[2,512,128]{2,1,0:T(8,128)(2,1)S(1)}, u32[]{:S(2)}, u32[]{:S(2)}) collective-permute-start(bf16[2,512,128]{2,1,0:T(8,128)(2,1)S(1)} %pad_maximum_fusion.2.refs_4_), channel_id=1, source_target_pairs={{0,5},{5,0},{1,4},{4,1},{2,7},{7,2},{3,6},{6,3},{8,13},{13,8},{9,1... | collective-permute-start | bytes 786440 | tf_op jit(solution)/shard_map/ppermute | solution.py:34
  37.5 10.0 %collective-permute-start.10 = (bf16[2,512,128]{2,1,0:T(8,128)(2,1)S(1)}, bf16[2,512,128]{2,1,0:T(8,128)(2,1)S(1)}, u32[]{:S(2)}, u32[]{:S(2)}) collective-permute-start(bf16[2,512,128]{2,1,0:T(8,128)(2,1)S(1)} %pad_maximum_fusion.3.refs_8_), channel_id=1, source_target_pairs={{0,24},{8,0},{16,8},{24,16},{1,25},{9,1},{17,9},{25,17},{2,26},{10... | collective-permute-start | bytes 786440 | tf_op jit(solution)/shard_map/ppermute | solution.py:26
  38.7 9.5 %collective-permute-start.2 = (bf16[2,512,128]{2,1,0:T(8,128)(2,1)S(1)}, bf16[2,512,128]{2,1,0:T(8,128)(2,1)S(1)}, u32[]{:S(2)}, u32[]{:S(2)}) collective-permute-start(bf16[2,512,128]{2,1,0:T(8,128)(2,1)S(1)} %pad_maximum_fusion.1.refs_0_), channel_id=1, source_target_pairs={{0,5},{5,0},{1,4},{4,1},{2,7},{7,2},{3,6},{6,3},{8,13},{13,8},{9,1... | collective-permute-start | bytes 786440 | tf_op jit(solution)/shard_map/ppermute | solution.py:34
  41.3 9.5 %collective-permute-start.12 = (bf16[2,512,128]{2,1,0:T(8,128)(2,1)S(1)}, bf16[2,512,128]{2,1,0:T(8,128)(2,1)S(1)}, u32[]{:S(2)}, u32[]{:S(2)}) collective-permute-start(bf16[2,512,128]{2,1,0:T(8,128)(2,1)S(1)} %pad_maximum_fusion.3.refs_8_), channel_id=1, source_target_pairs={{0,8},{8,16},{16,24},{24,0},{1,9},{9,17},{17,25},{25,1},{2,10},{10... | collective-permute-start | bytes 786440 | tf_op jit(solution)/shard_map/ppermute | solution.py:26
  43.0 36.1 %all-to-all-start.1 = ((bf16[8,256,256]{2,1,0:T(8,128)(2,1)}), bf16[8,256,256]{2,1,0:T(8,128)(2,1)}, u32[]{:S(2)}, u32[]{:S(2)}) async-start(bf16[8,256,256]{2,1,0:T(8,128)(2,1)} %broadcast_in_dim.7), calls=%async_computation.1 | async-start | bytes 2097152 | tf_op jit(solution)/shard_map/all_to_all | solution.py:172
  47.2 5.9 %collective-permute-start.1 = (bf16[2,512,128]{2,1,0:T(8,128)(2,1)S(1)}, bf16[2,512,128]{2,1,0:T(8,128)(2,1)S(1)}, u32[]{:S(2)}, u32[]{:S(2)}) collective-permute-start(bf16[2,512,128]{2,1,0:T(8,128)(2,1)S(1)} %pad_maximum_fusion.1.refs_0_), channel_id=1, source_target_pairs={{0,1},{1,0},{4,5},{5,4},{2,3},{3,2},{6,7},{7,6},{8,9},{9,8},{12,13... | collective-permute-start | bytes 786440 | tf_op jit(solution)/shard_map/ppermute | solution.py:30
  47.4 8.1 %collective-permute-start.17 = (bf16[2,512,128]{2,1,0:T(8,128)(2,1)S(1)}, bf16[2,512,128]{2,1,0:T(8,128)(2,1)S(1)}, u32[]{:S(2)}, u32[]{:S(2)}) collective-permute-start(bf16[2,512,128]{2,1,0:T(8,128)(2,1)S(1)} %collective-permute-done.16.refs_15_), channel_id=1, source_target_pairs={{0,8},{8,16},{16,24},{24,0},{1,9},{9,17},{17,25},{25,1},{2,10},{10... | collective-permute-start | bytes 786440 | tf_op jit(solution)/shard_map/ppermute | solution.py:26
  47.5 8.2 %collective-permute-start.8 = (bf16[2,512,128]{2,1,0:T(8,128)(2,1)S(1)}, bf16[2,512,128]{2,1,0:T(8,128)(2,1)}, u32[]{:S(2)}, u32[]{:S(2)}) collective-permute-start(bf16[2,512,128]{2,1,0:T(8,128)(2,1)S(1)} %collective-permute-done.6.refs_5_), channel_id=1, source_target_pairs={{0,5},{5,0},{1,4},{4,1},{2,7},{7,2},{3,6},{6,3},{8,13},{13,8},{9,1... | collective-permute-start | bytes 786440 | tf_op jit(solution)/shard_map/ppermute | solution.py:34
  48.2 7.5 %collective-permute-start.11 = (bf16[2,512,128]{2,1,0:T(8,128)(2,1)S(1)}, bf16[2,512,128]{2,1,0:T(8,128)(2,1)}, u32[]{:S(2)}, u32[]{:S(2)}) collective-permute-start(bf16[2,512,128]{2,1,0:T(8,128)(2,1)S(1)} %collective-permute-done.10.refs_9_), channel_id=1, source_target_pairs={{0,24},{8,0},{16,8},{24,16},{1,25},{9,1},{17,9},{25,17},{2,26},{10... | collective-permute-start | bytes 786440 | tf_op jit(solution)/shard_map/ppermute | solution.py:26
  50.8 5.5 %collective-permute-start.3 = (bf16[2,512,128]{2,1,0:T(8,128)(2,1)S(1)}, bf16[2,512,128]{2,1,0:T(8,128)(2,1)}, u32[]{:S(2)}, u32[]{:S(2)}) collective-permute-start(bf16[2,512,128]{2,1,0:T(8,128)(2,1)S(1)} %collective-permute-done.2.refs_2_), channel_id=1, source_target_pairs={{0,1},{1,0},{4,5},{5,4},{2,3},{3,2},{6,7},{7,6},{8,9},{9,8},{12,13... | collective-permute-start | bytes 786440 | tf_op jit(solution)/shard_map/ppermute | solution.py:30
  53.1 25.7 %copy-start.3 = (bf16[256,1024]{1,0:T(8,128)(2,1)S(1)}, bf16[256,1024]{1,0:T(8,128)(2,1)}, u32[]{:S(2)}) copy-start(bf16[256,1024]{1,0:T(8,128)(2,1)} %param.7) | copy-start | bytes 1572868
  65.4 1.4 copy-start.1
  66.8 12.8 %copy-start.2 = (bf16[1024,1024]{1,0:T(8,128)(2,1)S(1)}, bf16[1024,1024]{1,0:T(8,128)(2,1)}, u32[]{:S(2)}) copy-start(bf16[1024,1024]{1,0:T(8,128)(2,1)} %copy-done.1) | copy-start | bytes 6291460
  66.8 12.1 %collective-permute-start.18 = (f32[256,1024]{1,0:T(8,128)S(1)}, f32[256,1024]{1,0:T(8,128)S(1)}, u32[]{:S(2)}, u32[]{:S(2)}) collective-permute-start(f32[256,1024]{1,0:T(8,128)S(1)} %get-tuple-element.10), channel_id=1, source_target_pairs={{0,2},{2,0},{1,3},{3,1},{4,6},{6,4},{5,7},{7,5},{8,10},{10,8},{9,1... | collective-permute-start | bytes 3145736 | tf_op jit(solution)/shard_map/ppermute | solution.py:56
  79.1 2.0 %collective-permute-start.19 = (bf16[256,1024]{1,0:T(8,128)(2,1)S(1)}, bf16[256,1024]{1,0:T(8,128)(2,1)S(1)}, u32[]{:S(2)}, u32[]{:S(2)}) collective-permute-start(bf16[256,1024]{1,0:T(8,128)(2,1)S(1)} %multiply_convert_fusion), channel_id=1, source_target_pairs={{0,2},{2,0},{1,3},{3,1},{4,6},{6,4},{5,7},{7,5},{8,10},{10,8},{9,1... | collective-permute-start | bytes 1572872 | tf_op jit(solution)/shard_map/ppermute | solution.py:56
  83.1 36.0 %all-to-all-start.2 = ((bf16[8,2,16,8,256]{4,3,2,1,0:T(8,128)(2,1)}), bf16[8,2,16,8,256]{4,3,2,1,0:T(8,128)(2,1)S(1)}, u32[]{:S(2)}, u32[]{:S(2)}) async-start(bf16[8,2,16,8,256]{4,3,2,1,0:T(8,128)(2,1)} %pad_maximum_fusion), calls=%async_computation.2 | async-start | bytes 2097152 | tf_op jit(solution)/shard_map/all_to_all | solution.py:197
  89.8 31.2 %collective-permute-start.20 = (bf16[2048,256]{1,0:T(8,128)(2,1)}, bf16[2048,256]{1,0:T(8,128)(2,1)S(1)}, u32[]{:S(2)}, u32[]{:S(2)}) collective-permute-start(bf16[2048,256]{1,0:T(8,128)(2,1)} %bitcast.10), channel_id=1, source_target_pairs={{0,2},{2,0},{1,3},{3,1},{4,6},{6,4},{5,7},{7,5},{8,10},{10,8},{9,1... | collective-permute-start | bytes 3145736 | tf_op jit(solution)/shard_map/ppermute | solution.py:56
  136.5 2.9 %collective-permute-start.21 = (f32[8,2048]{1,0:T(8,128)S(1)}, f32[8,2048]{1,0:T(8,128)S(1)}, u32[]{:S(2)}, u32[]{:S(2)}) collective-permute-start(f32[8,2048]{1,0:T(8,128)S(1)} %get-tuple-element.23), channel_id=1, source_target_pairs={{0,2},{2,0},{1,3},{3,1},{4,6},{6,4},{5,7},{7,5},{8,10},{10,8},{9,1... | collective-permute-start | bytes 196616 | tf_op jit(solution)/shard_map/ppermute | solution.py:56

commit v2 on v1

--- a/solution.py
+++ b/solution.py
@@ -143,6 +143,66 @@
     )(spots, *pieces)
 
 
+def apply_kernel(place_ref, picked_ref, own_ref, other_ref, *refs):
+    outs, held_ref = refs[:-1], refs[-1]
+    rows = own_ref.shape[0]
+    groups, n, share, _ = held_ref.shape
+    for k, ref in enumerate((own_ref, other_ref)):
+        product = jnp.dot(ref[...], picked_ref[...], preferred_element_type=F32)
+        held_ref[:, :, :, k * rows : (k + 1) * rows] = product.T.reshape(groups, n, share, rows)
+    for k, out in enumerate(outs[:n]):
+        if k == n // 2:
+            half = groups // 2
+            spot = lax.rem(place_ref[0] + k, n)
+            out[...] = held_ref[:half, spot].astype(BF)
+            outs[n][...] = held_ref[half:, spot].astype(BF)
+        else:
+            out[...] = held_ref[:, lax.rem(place_ref[0] + k, n)].astype(BF)
+
+
+def applied_shares(place, picked, own, other, n, share):
+    rows, columns = own.shape[0], picked.shape[1]
+    groups = columns // (n * share)
+    vm = pl.BlockSpec(memory_space=pltpu.VMEM)
+    counts = [groups] * n + [groups // 2]
+    counts[n // 2] = groups // 2
+    return pl.pallas_call(
+        apply_kernel,
+        in_specs=[pl.BlockSpec(memory_space=pltpu.SMEM)] + [vm] * 3,
+        out_specs=[vm] * (n + 1),
+        out_shape=[jax.ShapeDtypeStruct((c, share, 2 * rows), BF) for c in counts],
+        scratch_shapes=[pltpu.VMEM((groups, n, share, 2 * rows), F32)],
+        compiler_params=pltpu.CompilerParams(vmem_limit_bytes=16 << 20),
+        cost_estimate=pl.CostEstimate(
+            flops=4 * rows * columns * own.shape[1], bytes_accessed=8 * rows * columns, transcendentals=0
+        ),
+        name="applied",
+    )(place, picked, own, other)
+
+
+def to_grid(x, step):
+    n = lax.axis_size("grid")
+    return lax.ppermute(x, "grid", [(i, (i + step) % n) for i in range(n)])
+
+
+def summed_on_grid(shares):
+    total = shares[0].astype(F32)
+    opposite = {1: shares[4], -1: shares[8]}
+    near = {1: shares[1], -1: shares[7]}
+    second = {1: shares[2], -1: shares[6]}
+    third = {1: shares[3], -1: shares[5]}
+    opposite = {way: to_grid(x, 3 * way) for way, x in opposite.items()}
+    third = {way: to_grid(x, 2 * way) for way, x in third.items()}
+    second = {way: to_grid(x, way) for way, x in second.items()}
+    sums = []
+    for way in (1, -1):
+        none = jnp.zeros_like(opposite[way])
+        both = [opposite[way], none] if way == 1 else [none, opposite[way]]
+        terms = near[way], second[way], third[way], jnp.concatenate(both)
+        sums.append(to_grid(sum(t.astype(F32) for t in terms).astype(BF), way))
+    return (total + sums[0].astype(F32) + sums[1].astype(F32)).astype(BF)
+
+
 def body(orbitals, points, fitting, screened):
     n_grid = lax.axis_size("grid")
     n_plane = lax.axis_size(PLANE)
@@ -186,24 +246,17 @@
     masked, fit_own = lax.optimization_barrier((masked, fit_own))
     masked_other = other_core(masked)
 
-    def applied_by(masked):
-        partial = lax.dot_general(
-            picked, masked, (((0,), (1,)), ((), ())), preferred_element_type=F32
-        ).astype(BF)
-        partial = partial.reshape(-1, n_grid, share, row_block)
-        return partial.transpose(1, 0, 2, 3)
-
-    partial = jnp.stack([applied_by(masked), applied_by(masked_other)], axis=1)
-    parts = lax.all_to_all(partial, "grid", 0, 0, tiled=True)
-    applied = jnp.sum(parts.astype(F32), axis=0).astype(BF)
-    applied = applied.reshape(2, 4, 2, 2 * share, row_block)
-    applied = jnp.where(xh == 0, applied, applied[:, :, ::-1])
+    applied = summed_on_grid(
+        applied_shares(grid_index[None], picked, masked, masked_other, n_grid, share)
+    )
+    applied = applied.reshape(4, 2, 2 * share, 2 * row_block)
+    applied = jnp.where(xh == 0, applied, applied[:, ::-1])
     applied = lax.dynamic_slice_in_dim(
-        jnp.concatenate([applied, applied], axis=1), lax.rem(4 - y, 4), 4, 1
-    ).reshape(2, -1, row_block)
+        jnp.concatenate([applied, applied]), lax.rem(4 - y, 4), 4, 0
+    ).reshape(-1, 2 * row_block)
     terms = sum(
         lax.dot_general(a, f, (((1,), (1,)), ((), ())), preferred_element_type=F32)
-        for a, f in ((applied[0], fit_own), (applied[1], fit_other))
+        for a, f in ((applied[:, :row_block], fit_own), (applied[:, row_block:], fit_other))
     ).astype(BF)
     parts = lax.all_to_all(terms.reshape(-1, share, nrows), CHIPS, 0, 0, tiled=True)
     exchange = -jnp.sum(parts.astype(F32), axis=0)

time: 156 us -> 159 us (1.019)
  starting transfers between devices: 43.4 us -> 53.4 us
  waiting for transfers between devices: 41.3 us -> 32.3 us
  local copies, waits for them, and re-layouts: 6.29 us -> 8.74 us
    all_to_all x1 -> x0, waiting for transfers between devices: 28.6 us -> none  [body(): parts = lax.all_to_all(partial, 'grid', 0, 0, tiled=True)]
    ppermute x0 -> x8, waiting for transfers between devices: none -> 17.3 us  [to_grid(): return lax.ppermute(x, 'grid', [(i, (i + step) % n) for i in range(n)])]
    ppermute x0 -> x8, starting transfers between devices: none -> 14.7 us  [to_grid(): return lax.ppermute(x, 'grid', [(i, (i + step) % n) for i in range(n)])]
    all_to_all x1 -> x0, starting transfers between devices: 6.72 us -> none  [body(): parts = lax.all_to_all(partial, 'grid', 0, 0, tiled=True)]
    ppermute x4, starting transfers between devices: 8.44 us -> 4.77 us  [with_mirror(): return lax.ppermute(x, X, [(0, 3), (3, 0), (1, 2), (2, 1)])]
    all_to_all x1, blocking collectives: 11.9 us -> 15.3 us  [body(): both = lax.all_to_all(both, ('grid', 'core'), 0, 0, tiled=True)]
    ppermute x4, starting transfers between devices: 12.9 us -> 16 us  [other_core(): return lax.ppermute(x, 'core', [(0, 1), (1, 0)])]
    all_to_all x1, blocking collectives: 14.9 us -> 12.4 us  [body(): lax.all_to_all(terms.reshape(-1, share, nrows), CHIPS, 0, 0, tiled=True)]
  transfers between devices with their start and end apart: 24 -> 31, of which waited for: 10 -> 11; matrix products, arithmetic and copies ran while one was open for 4% -> 4% of each run, Pallas kernels for 6% -> 6%
where the time goes in v2:
time: 159 us
  starting transfers between devices  53.4 us (34%)
  blocking collectives  47 us (30%)
  waiting for transfers between devices  32.3 us (20%)
  Pallas kernels  10.5 us (7%)
  local copies, waits for them, and re-layouts  8.74 us (5%)
  matrix products  5.02 us (3%)
    all_to_all x1, blocking collectives, sent_to_all(): return lax.all_to_all(copies, axis, split_axis=0, concat_axis=0, tiled=True)  19.3 us
    ppermute x8, waiting for transfers between devices, to_grid(): return lax.ppermute(x, 'grid', [(i, (i + step) % n) for i in range(n)])  17.3 us
    ppermute x4, starting transfers between devices, other_core(): return lax.ppermute(x, 'core', [(0, 1), (1, 0)])  16 us
    all_to_all x1, blocking collectives, body(): both = lax.all_to_all(both, ('grid', 'core'), 0, 0, tiled=True)  15.3 us
    ppermute x8, starting transfers between devices, to_grid(): return lax.ppermute(x, 'grid', [(i, (i + step) % n) for i in range(n)])  14.7 us
    all_to_all x1, blocking collectives, body(): lax.all_to_all(terms.reshape(-1, share, nrows), CHIPS, 0, 0, tiled=True)  12.4 us
    ppermute x9, starting transfers between devices, from_next(): return lax.ppermute(x, 'y', [(i, (i - step) % n) for i in range(n)])  9.77 us
    pallas_call x1, Pallas kernels, pick(): pl.pallas_call(pick_kernel, in_specs=[pl.BlockSpec(memory_space=pltpu.SME...  9.02 us
  transfers between devices with their start and end apart: 31, of which 11 were waited for; matrix products, arithmetic and copies ran while one was open for 4% of the time, Pallas kernels for 6%

profile of v2, /device:TPU:1, one launch (start us, length us, event | category | flops | bytes accessed | tf_op | source)
XLA Modules:
  0.0 158.9 jit_solution(3568547907984126514)
XLA Ops:
  0.6 0.8 copy-done
  1.5 19.3 %all_to_all.20 = bf16[8,128,128]{2,1,0:T(8,128)(2,1)S(1)} all-to-all(bf16[8,128,128]{2,1,0:T(8,128)(2,1)S(1)} %broadcast_in_dim.10), channel_id=1, replica_groups=mesh['grid'=8,'y'=4,'xh'=2,'core'=2,'pts'=2] {'grid'}, dimensions={0} | all-to-all | bytes 524288 | tf_op jit(solution)/shard_map/all_to_all | solution.py:21
  20.8 2.8 %collective-permute-start.14 = (bf16[512,128]{1,0:T(8,128)(2,1)S(1)}, bf16[512,128]{1,0:T(8,128)(2,1)S(1)}, u32[]{:S(2)}, u32[]{:S(2)}) collective-permute-start(bf16[512,128]{1,0:T(8,128)(2,1)S(1)} %bitcast.54), channel_id=1, source_target_pairs={{0,4},{4,0},{1,5},{5,1},{2,6},{6,2},{3,7},{7,3},{8,12},{12,8},{9,1... | collective-permute-start | bytes 393224 | tf_op jit(solution)/shard_map/ppermute | solution.py:38
  23.7 0.9 collective-permute-start.13
  24.5 2.9 %collective-permute-start.4 = (bf16[512,128]{1,0:T(8,128)(2,1)S(1)}, bf16[512,128]{1,0:T(8,128)(2,1)S(1)}, u32[]{:S(2)}, u32[]{:S(2)}) collective-permute-start(bf16[512,128]{1,0:T(8,128)(2,1)S(1)} %bitcast.50), channel_id=1, source_target_pairs={{0,16},{8,24},{16,0},{24,8},{1,17},{9,25},{17,1},{25,9},{2,18},{10... | collective-permute-start | bytes 393224 | tf_op jit(solution)/shard_map/ppermute | solution.py:26
  27.4 0.4 collective-permute-start.5
  27.8 2.3 %collective-permute-done.13 = bf16[512,128]{1,0:T(8,128)(2,1)S(1)} collective-permute-done((bf16[512,128]{1,0:T(8,128)(2,1)S(1)}, bf16[512,128]{1,0:T(8,128)(2,1)S(1)}, u32[]{:S(2)}, u32[]{:S(2)}) %collective-permute-start.13) | collective-permute-done | bytes 131104 | tf_op jit(solution)/shard_map/ppermute | solution.py:34
  30.1 1.4 collective-permute-start.16
  31.5 2.4 %collective-permute-done.5 = bf16[512,128]{1,0:T(8,128)(2,1)S(1)} collective-permute-done((bf16[512,128]{1,0:T(8,128)(2,1)S(1)}, bf16[512,128]{1,0:T(8,128)(2,1)S(1)}, u32[]{:S(2)}, u32[]{:S(2)}) %collective-permute-start.5) | collective-permute-done | bytes 131104 | tf_op jit(solution)/shard_map/ppermute | solution.py:26
  33.9 0.1 collective-permute-start.6
  34.0 0.1 collective-permute-start
  34.1 0.5 collective-permute-start.15
  34.6 1.5 collective-permute-start.7
  36.1 2.1 %collective-permute-done = bf16[512,128]{1,0:T(8,128)(2,1)S(1)} collective-permute-done((bf16[512,128]{1,0:T(8,128)(2,1)S(1)}, bf16[512,128]{1,0:T(8,128)(2,1)S(1)}, u32[]{:S(2)}, u32[]{:S(2)}) %collective-permute-start) | collective-permute-done | bytes 131104 | tf_op jit(solution)/shard_map/ppermute | solution.py:26
  38.2 0.9 collective-permute-start.10
  39.2 1.9 %collective-permute-start.2 = (bf16[2,512,128]{2,1,0:T(8,128)(2,1)S(1)}, bf16[2,512,128]{2,1,0:T(8,128)(2,1)S(1)}, u32[]{:S(2)}, u32[]{:S(2)}) collective-permute-start(bf16[2,512,128]{2,1,0:T(8,128)(2,1)S(1)} %pad_maximum_fusion.refs_0_), channel_id=1, source_target_pairs={{0,5},{5,0},{1,4},{4,1},{2,7},{7,2},{3,6},{6,3},{8,13},{13,8},{9,1... | collective-permute-start | bytes 786440 | tf_op jit(solution)/shard_map/ppermute | solution.py:34
  41.1 0.5 collective-permute-start.12
  41.6 2.0 %broadcast_in_dim.11 = bf16[8,256,256]{2,1,0:T(8,128)(2,1)} broadcast(bf16[256,256]{1,0:T(8,128)(2,1)} %param.6), dimensions={1,2} | broadcast | bytes 1179648 | tf_op jit(solution)/shard_map/broadcast_in_dim | solution.py:231
  43.7 4.2 %all-to-all-start.1 = ((bf16[8,256,256]{2,1,0:T(8,128)(2,1)}), bf16[8,256,256]{2,1,0:T(8,128)(2,1)}, u32[]{:S(2)}, u32[]{:S(2)}) async-start(bf16[8,256,256]{2,1,0:T(8,128)(2,1)} %broadcast_in_dim.11), calls=%async_computation.1 | async-start | bytes 2097152 | tf_op jit(solution)/shard_map/all_to_all | solution.py:232
  47.9 0.9 collective-permute-start.1
  48.8 0.6 collective-permute-start.17
  49.4 0.5 collective-permute-start.8
  49.9 2.4 %collective-permute-start.11 = (bf16[2,512,128]{2,1,0:T(8,128)(2,1)S(1)}, bf16[2,512,128]{2,1,0:T(8,128)(2,1)}, u32[]{:S(2)}, u32[]{:S(2)}) collective-permute-start(bf16[2,512,128]{2,1,0:T(8,128)(2,1)S(1)} %collective-permute-done.10.refs_9_), channel_id=1, source_target_pairs={{0,24},{8,0},{16,8},{24,16},{1,25},{9,1},{17,9},{25,17},{2,26},{10... | collective-permute-start | bytes 786440 | tf_op jit(solution)/shard_map/ppermute | solution.py:26
  52.3 0.1 collective-permute-start.3
  52.5 0.7 dynamic_slice.24
  53.2 0.8 fusion.20
  54.1 3.3 %collective-permute-done.17.refs_14_ = bf16[2,512,128]{2,1,0:T(8,128)(2,1)S(1)} collective-permute-done((bf16[2,512,128]{2,1,0:T(8,128)(2,1)S(1)}, bf16[2,512,128]{2,1,0:T(8,128)(2,1)S(1)}, u32[]{:S(2)}, u32[]{:S(2)}) %collective-permute-start.17) | collective-permute-done | bytes 262176 | tf_op jit(solution)/shard_map/ppermute | solution.py:26
  57.4 0.3 collective-permute-done.3.refs_3_
  57.7 9.0 %pick.1 = (f32[256,1024]{1,0:T(8,128)S(1)}, f32[256,1024]{1,0:T(8,128)S(1)}, bf16[1024,1024]{1,0:T(8,128)(2,1)S(1)}, bf16[4,2048,256]{2,1,0:T(8,128)(2,1)}) custom-call(s32[1536]{0:T(1024)S(1)} %fusion.13.spots_ref, bf16[2,512,128]{2,1,0:T(8,128)(2,1)S(1)} %pad_maximum_fusion.refs_0_, bf16[2,512,128]{2,1,0:T(8,128)(2,1)S(1)} %collective-permute-done.1.refs_1_, ...), custom_call_target="tpu_custom_call" | custom-call | flops 1073741824 | bytes 8388608 | tf_op jit(solution)/shard_map/pick/pallas_call | solution.py:121
  66.7 1.4 copy-done.1
  68.1 10.0 %collective-permute-start.18 = (f32[256,1024]{1,0:T(8,128)S(1)}, f32[256,1024]{1,0:T(8,128)S(1)}, u32[]{:S(2)}, u32[]{:S(2)}) collective-permute-start(f32[256,1024]{1,0:T(8,128)S(1)} %get-tuple-element.19), channel_id=1, source_target_pairs={{0,2},{2,0},{1,3},{3,1},{4,6},{6,4},{5,7},{7,5},{8,10},{10,8},{9,1... | collective-permute-start | bytes 3145736 | tf_op jit(solution)/shard_map/ppermute | solution.py:56
  78.0 2.3 %collective-permute-done.18 = f32[256,1024]{1,0:T(8,128)S(1)} collective-permute-done((f32[256,1024]{1,0:T(8,128)S(1)}, f32[256,1024]{1,0:T(8,128)S(1)}, u32[]{:S(2)}, u32[]{:S(2)}) %collective-permute-start.18) | collective-permute-done | bytes 1048608 | tf_op jit(solution)/shard_map/ppermute | solution.py:56
  80.3 0.3 multiply_convert_fusion.own_ref
  80.6 0.5 collective-permute-start.19
  81.1 1.5 collective-permute-done.19.other_ref
  82.6 1.6 %copy-done.2 = bf16[1024,1024]{1,0:T(8,128)(2,1)S(1)} copy-done((bf16[1024,1024]{1,0:T(8,128)(2,1)S(1)}, bf16[1024,1024]{1,0:T(8,128)(2,1)}, u32[]{:S(2)}) %copy-start.2) | copy-done | bytes 2097176
  84.2 1.5 applied.1
  85.7 1.6 %collective-permute-start.20 = (bf16[16,8,512]{2,1,0:T(8,128)(2,1)S(1)}, bf16[16,8,512]{2,1,0:T(8,128)(2,1)S(1)}, u32[]{:S(2)}, u32[]{:S(2)}) collective-permute-start(bf16[16,8,512]{2,1,0:T(8,128)(2,1)S(1)} %get-tuple-element.23), channel_id=1, source_target_pairs={{0,32},{32,64},{64,96},{96,128},{128,160},{160,192},{192,224},{224... | collective-permute-start | bytes 393224 | tf_op jit(solution)/shard_map/ppermute | solution.py:185
  87.3 2.1 %collective-permute-start.21 = (bf16[16,8,512]{2,1,0:T(8,128)(2,1)S(1)}, bf16[16,8,512]{2,1,0:T(8,128)(2,1)S(1)}, u32[]{:S(2)}, u32[]{:S(2)}) collective-permute-start(bf16[16,8,512]{2,1,0:T(8,128)(2,1)S(1)} %get-tuple-element.24), channel_id=1, source_target_pairs={{0,64},{32,96},{64,128},{96,160},{128,192},{160,224},{192,0},{224,... | collective-permute-start | bytes 393224 | tf_op jit(solution)/shard_map/ppermute | solution.py:185
  89.4 2.4 %collective-permute-start.22 = (bf16[8,8,512]{2,1,0:T(8,128)(2,1)S(1)}, bf16[8,8,512]{2,1,0:T(8,128)(2,1)S(1)}, u32[]{:S(2)}, u32[]{:S(2)}) collective-permute-start(bf16[8,8,512]{2,1,0:T(8,128)(2,1)S(1)} %get-tuple-element.25), channel_id=1, source_target_pairs={{0,96},{32,128},{64,160},{96,192},{128,224},{160,0},{192,32},{224,... | collective-permute-start | bytes 196616 | tf_op jit(solution)/shard_map/ppermute | solution.py:185
  91.8 1.2 collective-permute-start.28
  93.0 2.4 %collective-permute-start.24 = (bf16[16,8,512]{2,1,0:T(8,128)(2,1)S(1)}, bf16[16,8,512]{2,1,0:T(8,128)(2,1)S(1)}, u32[]{:S(2)}, u32[]{:S(2)}) collective-permute-start(bf16[16,8,512]{2,1,0:T(8,128)(2,1)S(1)} %get-tuple-element.27), channel_id=1, source_target_pairs={{0,224},{32,0},{64,32},{96,64},{128,96},{160,128},{192,160},{224,1... | collective-permute-start | bytes 393224 | tf_op jit(solution)/shard_map/ppermute | solution.py:185
  95.4 6.6 %collective-permute-done.22 = bf16[8,8,512]{2,1,0:T(8,128)(2,1)S(1)} collective-permute-done((bf16[8,8,512]{2,1,0:T(8,128)(2,1)S(1)}, bf16[8,8,512]{2,1,0:T(8,128)(2,1)S(1)}, u32[]{:S(2)}, u32[]{:S(2)}) %collective-permute-start.22) | collective-permute-done | bytes 65568 | tf_op jit(solution)/shard_map/ppermute | solution.py:185
  102.0 4.7 %collective-permute-start.25 = (bf16[16,8,512]{2,1,0:T(8,128)(2,1)S(1)}, bf16[16,8,512]{2,1,0:T(8,128)(2,1)S(1)}, u32[]{:S(2)}, u32[]{:S(2)}) collective-permute-start(bf16[16,8,512]{2,1,0:T(8,128)(2,1)S(1)} %get-tuple-element.28), channel_id=1, source_target_pairs={{0,192},{32,224},{64,0},{96,32},{128,64},{160,96},{192,128},{224,1... | collective-permute-start | bytes 393224 | tf_op jit(solution)/shard_map/ppermute | solution.py:185
  106.7 0.1 add_convert_fusion.2
  106.7 1.3 collective-permute-start.23
  108.0 6.9 %collective-permute-done.26 = bf16[8,8,512]{2,1,0:T(8,128)(2,1)S(1)} collective-permute-done((bf16[8,8,512]{2,1,0:T(8,128)(2,1)S(1)}, bf16[8,8,512]{2,1,0:T(8,128)(2,1)S(1)}, u32[]{:S(2)}, u32[]{:S(2)}) %collective-permute-start.26) | collective-permute-done | bytes 65568 | tf_op jit(solution)/shard_map/ppermute | solution.py:185
  114.9 0.1 add_convert_fusion.1
  115.0 0.3 collective-permute-start.27
  115.3 3.8 %collective-permute-done.27 = bf16[16,8,512]{2,1,0:T(8,128)(2,1)S(1)} collective-permute-done((bf16[16,8,512]{2,1,0:T(8,128)(2,1)S(1)}, bf16[16,8,512]{2,1,0:T(8,128)(2,1)S(1)}, u32[]{:S(2)}, u32[]{:S(2)}) %collective-permute-start.27) | collective-permute-done | bytes 131104 | tf_op jit(solution)/shard_map/ppermute | solution.py:185
  119.2 0.1 fusion.3
  119.3 1.7 %fusion.7 = f32[128,2048]{1,0:T(8,128)S(1)} fusion(bf16[2048,256]{1,0:T(8,128)(2,1)} %bitcast.11, bf16[128,512]{1,0:T(8,128)(2,1)S(1)} %bitcast.58), kind=kOutput, calls=%fused_computation.31 | convolution fusion | flops 134217728 | bytes 2162688 | tf_op jit(solution)/shard_map/dot_general | solution.py:258
  121.0 0.5 fusion.1
  121.5 12.4 %all_to_all.21 = bf16[16,8,2048]{2,1,0:T(8,128)(2,1)S(1)} all-to-all(bf16[16,8,2048]{2,1,0:T(8,128)(2,1)S(1)} %fusion.1), channel_id=1, replica_groups=mesh['grid'=8,'y'=4,'xh'=2,'core'=2,'pts'=2] {'y','xh','pts'}, dimensions={0} | all-to-all | bytes 1048576 | tf_op jit(solution)/shard_map/all_to_all | solution.py:261
  133.9 0.1 convert_reduce_fusion
  134.0 4.4 %collective-permute-start.29 = (f32[8,2048]{1,0:T(8,128)S(1)}, f32[8,2048]{1,0:T(8,128)S(1)}, u32[]{:S(2)}, u32[]{:S(2)}) collective-permute-start(f32[8,2048]{1,0:T(8,128)S(1)} %get-tuple-element.39), channel_id=1, source_target_pairs={{0,2},{2,0},{1,3},{3,1},{4,6},{6,4},{5,7},{7,5},{8,10},{10,8},{9,1... | collective-permute-start | bytes 196616 | tf_op jit(solution)/shard_map/ppermute | solution.py:56
  138.3 0.9 collective-permute-done.29
  139.3 0.3 rev.14
  139.6 0.1 fusion.4
  139.7 2.8 %fusion.2 = f32[4,2,2,8,128]{4,3,2,1,0:T(8,128)S(1)} fusion(bf16[16,2048,1]{1,0,2:T(8,128)(2,1)S(1)} %reshape.63, bf16[4,2048,256]{2,1,0:T(8,128)(2,1)} %get-tuple-element.31), kind=kOutput, calls=%fused_computation.4 | convolution fusion | flops 67125248 | bytes 4325376 | tf_op jit(solution)/shard_map/dot_general | solution.py:269
  142.6 0.1 reshape.58
  142.8 0.1 constant_dynamic-slice_fusion
  142.9 15.3 %all_to_all.22 = f32[16,2,8,128]{3,2,1,0:T(8,128)S(1)} all-to-all(f32[16,2,8,128]{3,2,1,0:T(8,128)S(1)} %copy.15), channel_id=1, replica_groups=mesh['grid'=8,'y'=4,'xh'=2,'core'=2,'pts'=2] {'grid','core'}, dimensions={0} | all-to-all | bytes 262144 | tf_op jit(solution)/shard_map/all_to_all | solution.py:280
  158.2 0.7 slice_bitcast_fusion
  (49 shorter events, 0.5 us)
Async XLA Ops:
  0.6 0.8 copy-start
  20.8 7.0 %collective-permute-start.14 = (bf16[512,128]{1,0:T(8,128)(2,1)S(1)}, bf16[512,128]{1,0:T(8,128)(2,1)S(1)}, u32[]{:S(2)}, u32[]{:S(2)}) collective-permute-start(bf16[512,128]{1,0:T(8,128)(2,1)S(1)} %bitcast.54), channel_id=1, source_target_pairs={{0,4},{4,0},{1,5},{5,1},{2,6},{6,2},{3,7},{7,3},{8,12},{12,8},{9,1... | collective-permute-start | bytes 393224 | tf_op jit(solution)/shard_map/ppermute | solution.py:38
  23.7 6.4 %collective-permute-start.13 = (bf16[512,128]{1,0:T(8,128)(2,1)S(1)}, bf16[512,128]{1,0:T(8,128)(2,1)S(1)}, u32[]{:S(2)}, u32[]{:S(2)}) collective-permute-start(bf16[512,128]{1,0:T(8,128)(2,1)S(1)} %bitcast.55), channel_id=1, source_target_pairs={{0,5},{5,0},{1,4},{4,1},{2,7},{7,2},{3,6},{6,3},{8,13},{13,8},{9,1... | collective-permute-start | bytes 393224 | tf_op jit(solution)/shard_map/ppermute | solution.py:34
  24.5 7.0 %collective-permute-start.4 = (bf16[512,128]{1,0:T(8,128)(2,1)S(1)}, bf16[512,128]{1,0:T(8,128)(2,1)S(1)}, u32[]{:S(2)}, u32[]{:S(2)}) collective-permute-start(bf16[512,128]{1,0:T(8,128)(2,1)S(1)} %bitcast.50), channel_id=1, source_target_pairs={{0,16},{8,24},{16,0},{24,8},{1,17},{9,25},{17,1},{25,9},{2,18},{10... | collective-permute-start | bytes 393224 | tf_op jit(solution)/shard_map/ppermute | solution.py:26
  27.4 6.4 %collective-permute-start.5 = (bf16[512,128]{1,0:T(8,128)(2,1)S(1)}, bf16[512,128]{1,0:T(8,128)(2,1)S(1)}, u32[]{:S(2)}, u32[]{:S(2)}) collective-permute-start(bf16[512,128]{1,0:T(8,128)(2,1)S(1)} %bitcast.51), channel_id=1, source_target_pairs={{0,8},{8,16},{16,24},{24,0},{1,9},{9,17},{17,25},{25,1},{2,10},{10... | collective-permute-start | bytes 393224 | tf_op jit(solution)/shard_map/ppermute | solution.py:26
  27.8 6.8 %collective-permute-start.9 = (bf16[512,128]{1,0:T(8,128)(2,1)S(1)}, bf16[512,128]{1,0:T(8,128)(2,1)S(1)}, u32[]{:S(2)}, u32[]{:S(2)}) collective-permute-start(bf16[512,128]{1,0:T(8,128)(2,1)S(1)} %bitcast.56), channel_id=1, source_target_pairs={{0,1},{1,0},{4,5},{5,4},{2,3},{3,2},{6,7},{7,6},{8,9},{9,8},{12,13... | collective-permute-start | bytes 393224 | tf_op jit(solution)/shard_map/ppermute | solution.py:30
  30.1 9.0 %collective-permute-start.16 = (bf16[2,512,128]{2,1,0:T(8,128)(2,1)S(1)}, bf16[2,512,128]{2,1,0:T(8,128)(2,1)S(1)}, u32[]{:S(2)}, u32[]{:S(2)}) collective-permute-start(bf16[2,512,128]{2,1,0:T(8,128)(2,1)S(1)} %pad_maximum_fusion.3.refs_12_), channel_id=1, source_target_pairs={{0,8},{8,16},{16,24},{24,0},{1,9},{9,17},{17,25},{25,1},{2,10},{10... | collective-permute-start | bytes 786440 | tf_op jit(solution)/shard_map/ppermute | solution.py:26
  33.9 7.2 %collective-permute-start.6 = (bf16[2,512,128]{2,1,0:T(8,128)(2,1)S(1)}, bf16[2,512,128]{2,1,0:T(8,128)(2,1)S(1)}, u32[]{:S(2)}, u32[]{:S(2)}) collective-permute-start(bf16[2,512,128]{2,1,0:T(8,128)(2,1)S(1)} %pad_maximum_fusion.1.refs_4_), channel_id=1, source_target_pairs={{0,1},{1,0},{4,5},{5,4},{2,3},{3,2},{6,7},{7,6},{8,9},{9,8},{12,13... | collective-permute-start | bytes 786440 | tf_op jit(solution)/shard_map/ppermute | solution.py:30
  34.0 4.2 %collective-permute-start = (bf16[512,128]{1,0:T(8,128)(2,1)S(1)}, bf16[512,128]{1,0:T(8,128)(2,1)S(1)}, u32[]{:S(2)}, u32[]{:S(2)}) collective-permute-start(bf16[512,128]{1,0:T(8,128)(2,1)S(1)} %bitcast.52), channel_id=1, source_target_pairs={{0,24},{8,0},{16,8},{24,16},{1,25},{9,1},{17,9},{25,17},{2,26},{10... | collective-permute-start | bytes 393224 | tf_op jit(solution)/shard_map/ppermute | solution.py:26
  34.1 13.8 %collective-permute-start.15 = (bf16[2,512,128]{2,1,0:T(8,128)(2,1)S(1)}, bf16[2,512,128]{2,1,0:T(8,128)(2,1)S(1)}, u32[]{:S(2)}, u32[]{:S(2)}) collective-permute-start(bf16[2,512,128]{2,1,0:T(8,128)(2,1)S(1)} %pad_maximum_fusion.3.refs_12_), channel_id=1, source_target_pairs={{0,24},{8,0},{16,8},{24,16},{1,25},{9,1},{17,9},{25,17},{2,26},{10... | collective-permute-start | bytes 786440 | tf_op jit(solution)/shard_map/ppermute | solution.py:26
  34.6 14.2 %collective-permute-start.7 = (bf16[2,512,128]{2,1,0:T(8,128)(2,1)S(1)}, bf16[2,512,128]{2,1,0:T(8,128)(2,1)S(1)}, u32[]{:S(2)}, u32[]{:S(2)}) collective-permute-start(bf16[2,512,128]{2,1,0:T(8,128)(2,1)S(1)} %pad_maximum_fusion.1.refs_4_), channel_id=1, source_target_pairs={{0,5},{5,0},{1,4},{4,1},{2,7},{7,2},{3,6},{6,3},{8,13},{13,8},{9,1... | collective-permute-start | bytes 786440 | tf_op jit(solution)/shard_map/ppermute | solution.py:34
  38.2 11.2 %collective-permute-start.10 = (bf16[2,512,128]{2,1,0:T(8,128)(2,1)S(1)}, bf16[2,512,128]{2,1,0:T(8,128)(2,1)S(1)}, u32[]{:S(2)}, u32[]{:S(2)}) collective-permute-start(bf16[2,512,128]{2,1,0:T(8,128)(2,1)S(1)} %pad_maximum_fusion.2.refs_8_), channel_id=1, source_target_pairs={{0,24},{8,0},{16,8},{24,16},{1,25},{9,1},{17,9},{25,17},{2,26},{10... | collective-permute-start | bytes 786440 | tf_op jit(solution)/shard_map/ppermute | solution.py:26
  39.2 10.7 %collective-permute-start.2 = (bf16[2,512,128]{2,1,0:T(8,128)(2,1)S(1)}, bf16[2,512,128]{2,1,0:T(8,128)(2,1)S(1)}, u32[]{:S(2)}, u32[]{:S(2)}) collective-permute-start(bf16[2,512,128]{2,1,0:T(8,128)(2,1)S(1)} %pad_maximum_fusion.refs_0_), channel_id=1, source_target_pairs={{0,5},{5,0},{1,4},{4,1},{2,7},{7,2},{3,6},{6,3},{8,13},{13,8},{9,1... | collective-permute-start | bytes 786440 | tf_op jit(solution)/shard_map/ppermute | solution.py:34
  41.1 11.3 %collective-permute-start.12 = (bf16[2,512,128]{2,1,0:T(8,128)(2,1)S(1)}, bf16[2,512,128]{2,1,0:T(8,128)(2,1)S(1)}, u32[]{:S(2)}, u32[]{:S(2)}) collective-permute-start(bf16[2,512,128]{2,1,0:T(8,128)(2,1)S(1)} %pad_maximum_fusion.2.refs_8_), channel_id=1, source_target_pairs={{0,8},{8,16},{16,24},{24,0},{1,9},{9,17},{17,25},{25,1},{2,10},{10... | collective-permute-start | bytes 786440 | tf_op jit(solution)/shard_map/ppermute | solution.py:26
  43.7 36.9 %all-to-all-start.1 = ((bf16[8,256,256]{2,1,0:T(8,128)(2,1)}), bf16[8,256,256]{2,1,0:T(8,128)(2,1)}, u32[]{:S(2)}, u32[]{:S(2)}) async-start(bf16[8,256,256]{2,1,0:T(8,128)(2,1)} %broadcast_in_dim.11), calls=%async_computation.1 | async-start | bytes 2097152 | tf_op jit(solution)/shard_map/all_to_all | solution.py:232
  47.9 6.2 %collective-permute-start.1 = (bf16[2,512,128]{2,1,0:T(8,128)(2,1)S(1)}, bf16[2,512,128]{2,1,0:T(8,128)(2,1)S(1)}, u32[]{:S(2)}, u32[]{:S(2)}) collective-permute-start(bf16[2,512,128]{2,1,0:T(8,128)(2,1)S(1)} %pad_maximum_fusion.refs_0_), channel_id=1, source_target_pairs={{0,1},{1,0},{4,5},{5,4},{2,3},{3,2},{6,7},{7,6},{8,9},{9,8},{12,13... | collective-permute-start | bytes 786440 | tf_op jit(solution)/shard_map/ppermute | solution.py:30
  48.8 8.6 %collective-permute-start.17 = (bf16[2,512,128]{2,1,0:T(8,128)(2,1)S(1)}, bf16[2,512,128]{2,1,0:T(8,128)(2,1)S(1)}, u32[]{:S(2)}, u32[]{:S(2)}) collective-permute-start(bf16[2,512,128]{2,1,0:T(8,128)(2,1)S(1)} %collective-permute-done.16.refs_15_), channel_id=1, source_target_pairs={{0,8},{8,16},{16,24},{24,0},{1,9},{9,17},{17,25},{25,1},{2,10},{10... | collective-permute-start | bytes 786440 | tf_op jit(solution)/shard_map/ppermute | solution.py:26
  49.4 8.0 %collective-permute-start.8 = (bf16[2,512,128]{2,1,0:T(8,128)(2,1)S(1)}, bf16[2,512,128]{2,1,0:T(8,128)(2,1)}, u32[]{:S(2)}, u32[]{:S(2)}) collective-permute-start(bf16[2,512,128]{2,1,0:T(8,128)(2,1)S(1)} %collective-permute-done.6.refs_5_), channel_id=1, source_target_pairs={{0,5},{5,0},{1,4},{4,1},{2,7},{7,2},{3,6},{6,3},{8,13},{13,8},{9,1... | collective-permute-start | bytes 786440 | tf_op jit(solution)/shard_map/ppermute | solution.py:34
  49.9 7.5 %collective-permute-start.11 = (bf16[2,512,128]{2,1,0:T(8,128)(2,1)S(1)}, bf16[2,512,128]{2,1,0:T(8,128)(2,1)}, u32[]{:S(2)}, u32[]{:S(2)}) collective-permute-start(bf16[2,512,128]{2,1,0:T(8,128)(2,1)S(1)} %collective-permute-done.10.refs_9_), channel_id=1, source_target_pairs={{0,24},{8,0},{16,8},{24,16},{1,25},{9,1},{17,9},{25,17},{2,26},{10... | collective-permute-start | bytes 786440 | tf_op jit(solution)/shard_map/ppermute | solution.py:26
  52.3 5.3 %collective-permute-start.3 = (bf16[2,512,128]{2,1,0:T(8,128)(2,1)S(1)}, bf16[2,512,128]{2,1,0:T(8,128)(2,1)}, u32[]{:S(2)}, u32[]{:S(2)}) collective-permute-start(bf16[2,512,128]{2,1,0:T(8,128)(2,1)S(1)} %collective-permute-done.2.refs_2_), channel_id=1, source_target_pairs={{0,1},{1,0},{4,5},{5,4},{2,3},{3,2},{6,7},{7,6},{8,9},{9,8},{12,13... | collective-permute-start | bytes 786440 | tf_op jit(solution)/shard_map/ppermute | solution.py:30
  52.5 27.9 %copy-start.3 = (bf16[256,1024]{1,0:T(8,128)(2,1)S(1)}, bf16[256,1024]{1,0:T(8,128)(2,1)}, u32[]{:S(2)}) copy-start(bf16[256,1024]{1,0:T(8,128)(2,1)} %param.7) | copy-start | bytes 1572868
  66.7 1.4 copy-start.1
  68.1 12.3 %collective-permute-start.18 = (f32[256,1024]{1,0:T(8,128)S(1)}, f32[256,1024]{1,0:T(8,128)S(1)}, u32[]{:S(2)}, u32[]{:S(2)}) collective-permute-start(f32[256,1024]{1,0:T(8,128)S(1)} %get-tuple-element.19), channel_id=1, source_target_pairs={{0,2},{2,0},{1,3},{3,1},{4,6},{6,4},{5,7},{7,5},{8,10},{10,8},{9,1... | collective-permute-start | bytes 3145736 | tf_op jit(solution)/shard_map/ppermute | solution.py:56
  80.6 2.0 %collective-permute-start.19 = (bf16[256,1024]{1,0:T(8,128)(2,1)S(1)}, bf16[256,1024]{1,0:T(8,128)(2,1)S(1)}, u32[]{:S(2)}, u32[]{:S(2)}) collective-permute-start(bf16[256,1024]{1,0:T(8,128)(2,1)S(1)} %multiply_convert_fusion.own_ref), channel_id=1, source_target_pairs={{0,2},{2,0},{1,3},{3,1},{4,6},{6,4},{5,7},{7,5},{8,10},{10,8},{9,1... | collective-permute-start | bytes 1572872 | tf_op jit(solution)/shard_map/ppermute | solution.py:56
  82.6 1.6 %copy-start.2 = (bf16[1024,1024]{1,0:T(8,128)(2,1)S(1)}, bf16[1024,1024]{1,0:T(8,128)(2,1)}, u32[]{:S(2)}) copy-start(bf16[1024,1024]{1,0:T(8,128)(2,1)} %copy-done.1) | copy-start | bytes 6291460
  85.7 21.0 %collective-permute-start.20 = (bf16[16,8,512]{2,1,0:T(8,128)(2,1)S(1)}, bf16[16,8,512]{2,1,0:T(8,128)(2,1)S(1)}, u32[]{:S(2)}, u32[]{:S(2)}) collective-permute-start(bf16[16,8,512]{2,1,0:T(8,128)(2,1)S(1)} %get-tuple-element.23), channel_id=1, source_target_pairs={{0,32},{32,64},{64,96},{96,128},{128,160},{160,192},{192,224},{224... | collective-permute-start | bytes 393224 | tf_op jit(solution)/shard_map/ppermute | solution.py:185
  87.3 19.4 %collective-permute-start.21 = (bf16[16,8,512]{2,1,0:T(8,128)(2,1)S(1)}, bf16[16,8,512]{2,1,0:T(8,128)(2,1)S(1)}, u32[]{:S(2)}, u32[]{:S(2)}) collective-permute-start(bf16[16,8,512]{2,1,0:T(8,128)(2,1)S(1)} %get-tuple-element.24), channel_id=1, source_target_pairs={{0,64},{32,96},{64,128},{96,160},{128,192},{160,224},{192,0},{224,... | collective-permute-start | bytes 393224 | tf_op jit(solution)/shard_map/ppermute | solution.py:185
  89.4 12.6 %collective-permute-start.22 = (bf16[8,8,512]{2,1,0:T(8,128)(2,1)S(1)}, bf16[8,8,512]{2,1,0:T(8,128)(2,1)S(1)}, u32[]{:S(2)}, u32[]{:S(2)}) collective-permute-start(bf16[8,8,512]{2,1,0:T(8,128)(2,1)S(1)} %get-tuple-element.25), channel_id=1, source_target_pairs={{0,96},{32,128},{64,160},{96,192},{128,224},{160,0},{192,32},{224,... | collective-permute-start | bytes 196616 | tf_op jit(solution)/shard_map/ppermute | solution.py:185
  91.8 29.2 %collective-permute-start.28 = (bf16[2048,256]{1,0:T(8,128)(2,1)}, bf16[2048,256]{1,0:T(8,128)(2,1)S(1)}, u32[]{:S(2)}, u32[]{:S(2)}) collective-permute-start(bf16[2048,256]{1,0:T(8,128)(2,1)} %bitcast.11), channel_id=1, source_target_pairs={{0,2},{2,0},{1,3},{3,1},{4,6},{6,4},{5,7},{7,5},{8,10},{10,8},{9,1... | collective-permute-start | bytes 3145736 | tf_op jit(solution)/shard_map/ppermute | solution.py:56
  93.0 21.9 %collective-permute-start.24 = (bf16[16,8,512]{2,1,0:T(8,128)(2,1)S(1)}, bf16[16,8,512]{2,1,0:T(8,128)(2,1)S(1)}, u32[]{:S(2)}, u32[]{:S(2)}) collective-permute-start(bf16[16,8,512]{2,1,0:T(8,128)(2,1)S(1)} %get-tuple-element.27), channel_id=1, source_target_pairs={{0,224},{32,0},{64,32},{96,64},{128,96},{160,128},{192,160},{224,1... | collective-permute-start | bytes 393224 | tf_op jit(solution)/shard_map/ppermute | solution.py:185
  102.0 13.0 %collective-permute-start.25 = (bf16[16,8,512]{2,1,0:T(8,128)(2,1)S(1)}, bf16[16,8,512]{2,1,0:T(8,128)(2,1)S(1)}, u32[]{:S(2)}, u32[]{:S(2)}) collective-permute-start(bf16[16,8,512]{2,1,0:T(8,128)(2,1)S(1)} %get-tuple-element.28), channel_id=1, source_target_pairs={{0,192},{32,224},{64,0},{96,32},{128,64},{160,96},{192,128},{224,1... | collective-permute-start | bytes 393224 | tf_op jit(solution)/shard_map/ppermute | solution.py:185
  106.7 8.3 %collective-permute-start.26 = (bf16[8,8,512]{2,1,0:T(8,128)(2,1)S(1)}, bf16[8,8,512]{2,1,0:T(8,128)(2,1)S(1)}, u32[]{:S(2)}, u32[]{:S(2)}) collective-permute-start(bf16[8,8,512]{2,1,0:T(8,128)(2,1)S(1)} %get-tuple-element.29), channel_id=1, source_target_pairs={{0,160},{32,192},{64,224},{96,0},{128,32},{160,64},{192,96},{224,1... | collective-permute-start | bytes 196616 | tf_op jit(solution)/shard_map/ppermute | solution.py:185
  106.7 8.6 %collective-permute-start.23 = (bf16[16,8,512]{2,1,0:T(8,128)(2,1)S(1)}, bf16[16,8,512]{2,1,0:T(8,128)(2,1)S(1)}, u32[]{:S(2)}, u32[]{:S(2)}) collective-permute-start(bf16[16,8,512]{2,1,0:T(8,128)(2,1)S(1)} %add_convert_fusion.2), channel_id=1, source_target_pairs={{0,32},{32,64},{64,96},{96,128},{128,160},{160,192},{192,224},{224... | collective-permute-start | bytes 393224 | tf_op jit(solution)/shard_map/ppermute | solution.py:185
  115.0 4.1 %collective-permute-start.27 = (bf16[16,8,512]{2,1,0:T(8,128)(2,1)S(1)}, bf16[16,8,512]{2,1,0:T(8,128)(2,1)S(1)}, u32[]{:S(2)}, u32[]{:S(2)}) collective-permute-start(bf16[16,8,512]{2,1,0:T(8,128)(2,1)S(1)} %add_convert_fusion.1), channel_id=1, source_target_pairs={{0,224},{32,0},{64,32},{96,64},{128,96},{160,128},{192,160},{224,1... | collective-permute-start | bytes 393224 | tf_op jit(solution)/shard_map/ppermute | solution.py:185
  134.0 5.3 %collective-permute-start.29 = (f32[8,2048]{1,0:T(8,128)S(1)}, f32[8,2048]{1,0:T(8,128)S(1)}, u32[]{:S(2)}, u32[]{:S(2)}) collective-permute-start(f32[8,2048]{1,0:T(8,128)S(1)} %get-tuple-element.39), channel_id=1, source_target_pairs={{0,2},{2,0},{1,3},{3,1},{4,6},{6,4},{5,7},{7,5},{8,10},{10,8},{9,1... | collective-permute-start | bytes 196616 | tf_op jit(solution)/shard_map/ppermute | solution.py:56
